TPU v7x, 32 devices: a whole 2x2x4 slice. The times are simulated.
32 devices in a mesh: row: 8 (over z, x), col: 4 (over y, core).
Axes of the slice: x: 2, y: 2, z: 4, core: 2. Of those that a mesh axis runs over, the one named last changes fastest.
Arguments:
- hidden_in: bfloat16 [32, 512, 1024], P('row', 'col'), may hold values from -6 to 6
- first_values: bfloat16 [32, 1024, 512], P('row', 'col'), may hold values from -6 to 6
- lengths: int32 [32, 4], P('row'), may hold values from 1 to 256, 512 in all within a row
- places: int32 [32, 512], P('row'), may hold values from 0 to 511, each once within a row
- gain_attn: float32 [1024], replicated, may hold values from 0.1 to 1.9
- gain_ffn: float32 [1024], replicated, may hold values from 0.1 to 1.9
- w_query: bfloat16 [1024, 1024], P('row', 'col'), may hold values from -0.1875 to 0.1875
- w_key: bfloat16 [1024, 1024], P('row', 'col'), may hold values from -0.1875 to 0.1875
- w_value: bfloat16 [1024, 1024], P('row', 'col'), may hold values from -0.1875 to 0.1875
- w_out: bfloat16 [1024, 1024], P('col', 'row'), may hold values from -3 to 3
- w_gate: bfloat16 [1024, 2816], P('row', 'col'), may hold values from -0.1875 to 0.1875
- w_up: bfloat16 [1024, 2816], P('row', 'col'), may hold values from -0.1875 to 0.1875
- w_down: bfloat16 [2816, 1024], P('col', 'row'), may hold values from -0.109375 to 0.109375
- out_grad: bfloat16 [32, 512, 1024], P('row', 'col'), may hold values from -6 to 6
Outputs:
- layer_out: bfloat16 [32, 512, 1024], P('row', 'col')
- grad_hidden: float32 [32, 512, 1024], P('row', 'col')
- grad_first_values: float32 [32, 1024, 512], P('row', 'col')
- grad_gain_attn: float32 [1024], replicated
- grad_gain_ffn: float32 [1024], replicated
- grad_w_query: float32 [1024, 1024], P('row', 'col')
- grad_w_key: float32 [1024, 1024], P('row', 'col')
- grad_w_value: float32 [1024, 1024], P('row', 'col')
- grad_w_out: float32 [1024, 1024], P('col', 'row')
- grad_w_gate: float32 [1024, 2816], P('row', 'col')
- grad_w_up: float32 [1024, 2816], P('row', 'col')
- grad_w_down: float32 [2816, 1024], P('col', 'row')
Inputs may be any that keep to these rules, and one draw needn't show every extreme that they name: Each row of lengths sums to 512; the largest length in the draw is 256. Each row of places holds every number of 0 to 511 once.
All inputs are finite; a program needn't handle non-finite values.
Results may differ from a plain program's by a relative error of at most 0.015.
Values may be sent and summed in bfloat16 or wider, within the bound.
A program may use at most 192 MiB of HBM per device.

v0:
```python
import jax
import jax.numpy as jnp
from jax import lax
from jax.sharding import PartitionSpec as P

D = 1024
HEAD_DIM = 64
TOK_MB = 512
MICRO = 4


EPSILON = 1e-06
MASKED = -1e30


def product(left, right):
    return jnp.dot(left, right, preferred_element_type=jnp.float32)


def product_left(left, right):
    return lax.dot_general(
        left, right, (((0,), (0,)), ((), ())), preferred_element_type=jnp.float32
    )


def product_right(left, right):
    return lax.dot_general(
        left, right, (((1,), (1,)), ((), ())), preferred_element_type=jnp.float32
    )


def token_places(lengths_row, count):
    ends_at = jnp.cumsum(lengths_row)
    index_row = jnp.arange(count, dtype=jnp.int32)
    segment_id = jnp.sum((index_row[:, None] >= ends_at[None, :]).astype(jnp.int32), axis=1)
    starts_at = ends_at - lengths_row
    one_hot = segment_id[:, None] == jnp.arange(lengths_row.shape[0], dtype=jnp.int32)[None, :]
    position = index_row - jnp.sum(jnp.where(one_hot, starts_at[None, :], 0), axis=1)
    return (segment_id, position)


def rotary_tables(position):
    half_dim = HEAD_DIM // 2
    freq_index = jnp.arange(half_dim, dtype=jnp.float32)
    inverse = 10000.0 ** (-freq_index / half_dim)
    angles = position.astype(jnp.float32)[:, None] * inverse[None, :]
    return (jnp.cos(angles)[:, None, :], jnp.sin(angles)[:, None, :])


def rotate(field, cosine, sine):
    half_dim = field.shape[-1] // 2
    first_half, second_half = (field[..., :half_dim], field[..., half_dim:])
    return jnp.concatenate(
        [first_half * cosine - second_half * sine, second_half * cosine + first_half * sine],
        axis=-1,
    )


def rotate_back(field, cosine, sine):
    half_dim = field.shape[-1] // 2
    first_half, second_half = (field[..., :half_dim], field[..., half_dim:])
    return jnp.concatenate(
        [first_half * cosine + second_half * sine, second_half * cosine - first_half * sine],
        axis=-1,
    )


def spread_tokens(values):
    return lax.all_gather(values, "col", axis=0, tiled=True)


def reduce_tokens(values):
    return lax.psum_scatter(values, "col", scatter_dimension=0, tiled=True)


def body(
    hidden_in,
    first_values,
    lengths,
    places,
    gain_attn,
    gain_ffn,
    w_query,
    w_key,
    w_value,
    w_out,
    w_gate,
    w_up,
    w_down,
    out_grad,
):
    width_col = w_query.shape[1]
    heads_col = width_col // HEAD_DIM
    block_rows = min(512, TOK_MB)
    block_count = TOK_MB // block_rows
    local_rows = hidden_in.shape[1]
    row_start = lax.axis_index("col") * local_rows
    score_scale = HEAD_DIM ** (-0.5)
    tiles = (w_query, w_key, w_value, w_out, w_gate, w_up, w_down)

    def own_rows(values):
        return lax.dynamic_slice_in_dim(values, row_start, local_rows)

    hidden_width = w_gate.shape[1]
    full_shapes = (
        (D, width_col),
        (D, width_col),
        (D, width_col),
        (width_col, D),
        (D, hidden_width),
        (D, hidden_width),
        (hidden_width, D),
    )
    grads_full = tuple((jnp.zeros(shape_item, jnp.float32) for shape_item in full_shapes))
    grads_tile = tuple((jnp.zeros(tile_item.shape, jnp.float32) for tile_item in tiles))
    gain_sum_one = jnp.zeros((D,), jnp.float32)
    gain_sum_two = jnp.zeros((D,), jnp.float32)
    out_pieces, input_pieces, value_pieces = ([], [], [])
    for micro_step in range(MICRO):
        gathered = (
            lax.all_gather(tiles[0], "row", axis=0, tiled=True),
            lax.all_gather(tiles[1], "row", axis=0, tiled=True),
            lax.all_gather(tiles[2], "row", axis=0, tiled=True),
            lax.all_gather(tiles[3], "row", axis=1, tiled=True),
            lax.all_gather(tiles[4], "row", axis=0, tiled=True),
            lax.all_gather(tiles[5], "row", axis=0, tiled=True),
            lax.all_gather(tiles[6], "row", axis=1, tiled=True),
        )
        wq_all, wk_all, wv_all, wo_all, wg_all, wu_all, wd_all = gathered
        places_mb = places[micro_step]
        packed_order = (
            jnp.zeros((TOK_MB,), jnp.int32).at[places_mb].set(jnp.arange(TOK_MB, dtype=jnp.int32))
        )
        stored_hidden, stored_grad = (
            lax.all_gather(hidden_in[micro_step], "col", axis=0, tiled=True),
            lax.all_gather(out_grad[micro_step], "col", axis=0, tiled=True),
        )
        hidden_full = jnp.take(stored_hidden, packed_order, axis=0).astype(jnp.float32)
        grad_full_rows = jnp.take(stored_grad, packed_order, axis=0)
        first_mb = jnp.take(jnp.transpose(first_values[micro_step]), packed_order, axis=0).astype(
            jnp.float32
        )
        hidden_mb = own_rows(hidden_full)
        grad_mb = own_rows(grad_full_rows)
        segment_id, position = token_places(lengths[micro_step], TOK_MB)
        cosine, sine = rotary_tables(position)
        token_index = jnp.arange(TOK_MB, dtype=jnp.int32)
        scale_full = lax.rsqrt(jnp.mean(hidden_full * hidden_full, axis=1, keepdims=True) + EPSILON)
        scale_one = own_rows(scale_full)
        normed_one = (hidden_full * scale_full * gain_attn).astype(jnp.bfloat16)
        query_raw = product(normed_one, wq_all).reshape(TOK_MB, heads_col, HEAD_DIM)
        key_raw = product(normed_one, wk_all).reshape(TOK_MB, heads_col, HEAD_DIM)
        queries = rotate(query_raw, cosine, sine).astype(jnp.bfloat16)
        keys = rotate(key_raw, cosine, sine).astype(jnp.bfloat16)
        values = (
            (0.5 * product(normed_one, wv_all) + 0.5 * first_mb)
            .astype(jnp.bfloat16)
            .reshape(TOK_MB, heads_col, HEAD_DIM)
        )

        def block_scores(start_row):
            query_index = start_row + jnp.arange(block_rows, dtype=jnp.int32)
            allowed = (segment_id[:, None] == segment_id[None, :]) & (
                query_index[:, None] >= token_index[None, :]
            )
            raw_scores = (
                jnp.einsum("qhd,khd->hqk", queries, keys, preferred_element_type=jnp.float32)
                * score_scale
            )
            return (queries, jnp.where(allowed[None], raw_scores, MASKED))

        def attend(block_index):
            query_block, scores = block_scores(block_index * block_rows)
            row_top = jnp.max(scores, axis=-1, keepdims=True)
            log_total = row_top + jnp.log(
                jnp.sum(jnp.exp(scores - row_top), axis=-1, keepdims=True)
            )
            probs = jnp.exp(scores - log_total).astype(jnp.bfloat16)
            mixed = jnp.einsum("hqk,khd->qhd", probs, values, preferred_element_type=jnp.float32)
            return (mixed.astype(jnp.bfloat16), log_total[..., 0])

        attended, log_totals = lax.map(attend, jnp.arange(block_count, dtype=jnp.int32))
        attended = attended.reshape(TOK_MB, width_col)
        mid_mb = hidden_mb + reduce_tokens(product(attended, wo_all))
        scale_two = lax.rsqrt(jnp.mean(mid_mb * mid_mb, axis=1, keepdims=True) + EPSILON)
        normed_two = spread_tokens((mid_mb * scale_two * gain_ffn).astype(jnp.bfloat16))
        gate_raw = product(normed_two, wg_all)
        up_raw = product(normed_two, wu_all)
        sigmoid_gate = jax.nn.sigmoid(gate_raw)
        silu_gate = gate_raw * sigmoid_gate
        hidden_act = (silu_gate * up_raw).astype(jnp.bfloat16)
        packed_out = (mid_mb + reduce_tokens(product(hidden_act, wd_all))).astype(jnp.bfloat16)
        grad_down = product_left(hidden_act, grad_full_rows)
        d_hidden = product_right(grad_full_rows, wd_all)
        d_gate = (
            d_hidden * up_raw * sigmoid_gate * (1.0 + gate_raw * (1.0 - sigmoid_gate))
        ).astype(jnp.bfloat16)
        d_up = (d_hidden * silu_gate).astype(jnp.bfloat16)
        grad_gate = product_left(normed_two, d_gate)
        grad_up = product_left(normed_two, d_up)
        d_normed_two = reduce_tokens(product_right(d_gate, wg_all) + product_right(d_up, wu_all))
        gain_sum_two = gain_sum_two + jnp.sum(d_normed_two * mid_mb * scale_two, axis=0)
        scaled_two = d_normed_two * gain_ffn
        stat_two = jnp.sum(scaled_two * mid_mb, axis=1, keepdims=True)
        d_mid = (
            grad_mb.astype(jnp.float32)
            + scale_two * scaled_two
            - mid_mb * (scale_two * scale_two * scale_two * stat_two / D)
        )
        d_branch = spread_tokens(d_mid.astype(jnp.bfloat16))
        grad_out = product_left(attended, d_branch)
        d_attended = (
            product_right(d_branch, wo_all)
            .astype(jnp.bfloat16)
            .reshape(TOK_MB, heads_col, HEAD_DIM)
        )

        def attend_back(carry, block_index):
            key_acc, value_acc = carry
            start_row = block_index * block_rows
            query_block, scores = block_scores(start_row)
            log_block = log_totals[block_index]
            probs = jnp.exp(scores - log_block[..., None])
            d_probs = jnp.einsum(
                "qhd,khd->hqk", d_attended, values, preferred_element_type=jnp.float32
            )
            inner_sum = jnp.sum(probs * d_probs, axis=-1, keepdims=True)
            d_scores = (probs * (d_probs - inner_sum)).astype(jnp.bfloat16)
            d_query = (
                jnp.einsum("hqk,khd->qhd", d_scores, keys, preferred_element_type=jnp.float32)
                * score_scale
            )
            key_acc = (
                key_acc
                + jnp.einsum(
                    "hqk,qhd->khd", d_scores, query_block, preferred_element_type=jnp.float32
                )
                * score_scale
            )
            value_acc = value_acc + jnp.einsum(
                "hqk,qhd->khd",
                probs.astype(jnp.bfloat16),
                d_attended,
                preferred_element_type=jnp.float32,
            )
            return ((key_acc, value_acc), d_query)

        empty_heads = jnp.zeros((TOK_MB, heads_col, HEAD_DIM), jnp.float32)
        (key_grads, value_grads), query_grads = lax.scan(
            attend_back, (empty_heads, empty_heads), jnp.arange(block_count, dtype=jnp.int32)
        )
        d_values = value_grads.astype(jnp.bfloat16).reshape(TOK_MB, width_col)
        half_values = 0.5 * d_values.astype(jnp.float32)
        value_pieces.append(jnp.transpose(jnp.take(half_values, places_mb, axis=0)))
        d_value_proj = half_values.astype(jnp.bfloat16)
        d_query_raw = (
            rotate_back(query_grads.reshape(TOK_MB, heads_col, HEAD_DIM), cosine, sine)
            .astype(jnp.bfloat16)
            .reshape(TOK_MB, width_col)
        )
        d_key_raw = (
            rotate_back(key_grads, cosine, sine).astype(jnp.bfloat16).reshape(TOK_MB, width_col)
        )
        grad_query = product_left(normed_one, d_query_raw)
        grad_key = product_left(normed_one, d_key_raw)
        grad_value = product_left(normed_one, d_value_proj)
        d_normed_one = reduce_tokens(
            product_right(d_query_raw, wq_all)
            + product_right(d_key_raw, wk_all)
            + product_right(d_value_proj, wv_all)
        )
        gain_sum_one = gain_sum_one + jnp.sum(d_normed_one * hidden_mb * scale_one, axis=0)
        scaled_one = d_normed_one * gain_attn
        stat_one = jnp.sum(scaled_one * hidden_mb, axis=1, keepdims=True)
        packed_input = (
            d_mid
            + scale_one * scaled_one
            - hidden_mb * (scale_one * scale_one * scale_one * stat_one / D)
        )
        out_whole, input_whole = (
            lax.all_gather(
                packed_out.astype(jnp.float32).astype(jnp.bfloat16), "col", axis=0, tiled=True
            ).astype(jnp.float32),
            lax.all_gather(packed_input.astype(jnp.bfloat16), "col", axis=0, tiled=True).astype(
                packed_input.dtype
            ),
        )
        stored_places = lax.dynamic_slice_in_dim(places_mb, row_start, local_rows)
        out_pieces.append(jnp.take(out_whole, stored_places, axis=0).astype(jnp.bfloat16))
        input_pieces.append(jnp.take(input_whole, stored_places, axis=0))
        new_grads = (grad_query, grad_key, grad_value, grad_out, grad_gate, grad_up, grad_down)
        grads_full = tuple((earlier + later for earlier, later in zip(grads_full, new_grads)))
    grads_tile = (
        lax.psum_scatter(
            grads_full[0].astype(jnp.bfloat16), "row", scatter_dimension=0, tiled=True
        ).astype(jnp.float32),
        lax.psum_scatter(
            grads_full[1].astype(jnp.bfloat16), "row", scatter_dimension=0, tiled=True
        ).astype(jnp.float32),
        lax.psum_scatter(
            grads_full[2].astype(jnp.bfloat16), "row", scatter_dimension=0, tiled=True
        ).astype(jnp.float32),
        lax.psum_scatter(
            grads_full[3].astype(jnp.bfloat16), "row", scatter_dimension=1, tiled=True
        ).astype(jnp.float32),
        lax.psum_scatter(
            grads_full[4].astype(jnp.bfloat16), "row", scatter_dimension=0, tiled=True
        ).astype(jnp.float32),
        lax.psum_scatter(
            grads_full[5].astype(jnp.bfloat16), "row", scatter_dimension=0, tiled=True
        ).astype(jnp.float32),
        lax.psum_scatter(
            grads_full[6].astype(jnp.bfloat16), "row", scatter_dimension=1, tiled=True
        ).astype(jnp.float32),
    )
    gain_grad_one, gain_grad_two = lax.psum((gain_sum_one, gain_sum_two), ("row", "col"))
    return (
        jnp.stack(out_pieces, axis=0),
        jnp.stack(input_pieces, axis=0),
        jnp.stack(value_pieces, axis=0),
        gain_grad_one,
        gain_grad_two,
        grads_tile[0],
        grads_tile[1],
        grads_tile[2],
        grads_tile[3],
        grads_tile[4],
        grads_tile[5],
        grads_tile[6],
    )


def solution(mesh):
    return jax.shard_map(
        body,
        mesh=mesh,
        in_specs=(
            P("row", "col", None),
            P("row", "col", None),
            P("row", None),
            P("row", None),
            P(),
            P(),
            P("row", "col"),
            P("row", "col"),
            P("row", "col"),
            P("col", "row"),
            P("row", "col"),
            P("row", "col"),
            P("col", "row"),
            P("row", "col", None),
        ),
        out_specs=(
            P("row", "col", None),
            P("row", "col", None),
            P("row", "col", None),
            P(),
            P(),
            P("row", "col"),
            P("row", "col"),
            P("row", "col"),
            P("col", "row"),
            P("row", "col"),
            P("row", "col"),
            P("col", "row"),
        ),
        check_vma=False,
    )
```

profile of v0, /device:TPU:0, one launch (start us, length us, event | category | flops | bytes accessed | tf_op | source)
XLA Modules:
  0.0 1710.5 jit_solution(1301464961985849624)
XLA Ops:
  24.7 33.2 %all_gather.116 = bf16[1024,256]{1,0:T(8,128)(2,1)S(1)} all-gather(bf16[128,256]{1,0:T(8,128)(2,1)S(1)} %copy-done.200), channel_id=1, replica_groups=mesh['row'=8,'col'=4] {'row'}, dimensions={0}, use_global_device_ids=true | all-gather | bytes 589824 | tf_op jit(solution)/shard_map/all_gather | solution.py:121
  59.1 31.5 %all_gather.117 = bf16[1024,256]{1,0:T(8,128)(2,1)S(1)} all-gather(bf16[128,256]{1,0:T(8,128)(2,1)S(1)} %copy-done.201), channel_id=1, replica_groups=mesh['row'=8,'col'=4] {'row'}, dimensions={0}, use_global_device_ids=true | all-gather | bytes 589824 | tf_op jit(solution)/shard_map/all_gather | solution.py:122
  90.7 33.4 %all_gather.115 = bf16[1024,256]{1,0:T(8,128)(2,1)} all-gather(bf16[128,256]{1,0:T(8,128)(2,1)S(1)} %copy-done.202), channel_id=1, replica_groups=mesh['row'=8,'col'=4] {'row'}, dimensions={0}, use_global_device_ids=true | all-gather | bytes 589824 | tf_op jit(solution)/shard_map/all_gather | solution.py:123
  125.0 28.3 %all_gather.118 = bf16[256,1024]{1,0:T(8,128)(2,1)} all-gather(bf16[256,128]{1,0:T(8,128)(2,1)S(1)} %copy-done.203), channel_id=1, replica_groups=mesh['row'=8,'col'=4] {'row'}, dimensions={1}, use_global_device_ids=true | all-gather | bytes 589824 | tf_op jit(solution)/shard_map/all_gather | solution.py:124
  168.3 4.1 gather_fusion.6
  174.1 4.1 gather_fusion.9
  179.3 4.1 multiply_convert_fusion.7
  192.5 4.8 gather_fusion.12
  201.2 21.0 %reduce-scatter.32.cloned.1.call-done = f32[128,1024]{1,0:T(8,128)} async-done(((f32[512,1024]{1,0:T(8,128)}), f32[128,1024]{1,0:T(8,128)}) %reduce-scatter.32.cloned.1.call-update) | async-done | bytes 524304 | tf_op jit(solution)/shard_map/reduce_scatter | solution.py:73
  226.6 40.7 %all-gather.38.cloned.1.call-done = bf16[1024,704]{0,1:T(8,128)(2,1)} async-done(((bf16[128,704]{0,1:T(8,128)(2,1)}), bf16[1024,704]{0,1:T(8,128)(2,1)}) %all-gather.38.cloned.1.call-update) | async-done | bytes 1441808 | tf_op jit(solution)/shard_map/all_gather | solution.py:125
  267.3 17.1 all-gather.36.cloned.1.call-done
  288.1 41.3 %all-gather.40.cloned.1.call-done = bf16[1024,704]{0,1:T(8,128)(2,1)} async-done(((bf16[128,704]{0,1:T(8,128)(2,1)}), bf16[1024,704]{0,1:T(8,128)(2,1)}) %all-gather.40.cloned.1.call-update) | async-done | bytes 1441808 | tf_op jit(solution)/shard_map/all_gather | solution.py:126
  333.1 39.4 %all-gather.42.cloned.1.call-done = bf16[704,1024]{1,0:T(8,128)(2,1)} async-done(((bf16[704,128]{1,0:T(8,128)(2,1)}), bf16[704,1024]{1,0:T(8,128)(2,1)}) %all-gather.42.cloned.1.call-update) | async-done | bytes 1441808 | tf_op jit(solution)/shard_map/all_gather | solution.py:127
  372.5 5.0 multiply_convert_fusion.14
  381.8 29.5 %reduce-scatter.48.cloned.1.call-done = f32[128,1024]{1,0:T(8,128)} async-done(((f32[512,1024]{1,0:T(8,128)}), f32[128,1024]{1,0:T(8,128)}) %reduce-scatter.48.cloned.1.call-update) | async-done | bytes 524304 | tf_op jit(solution)/shard_map/reduce_scatter | solution.py:73
  478.4 4.8 gather_fusion.18
  483.3 4.8 gather_fusion.16
  488.1 4.9 gather_fusion.14
  499.7 20.8 %reduce-scatter.36.cloned.1.call-done = f32[128,1024]{1,0:T(8,128)} async-done(((f32[512,1024]{1,0:T(8,128)}), f32[128,1024]{1,0:T(8,128)}) %reduce-scatter.36.cloned.1.call-update) | async-done | bytes 524304 | tf_op jit(solution)/shard_map/reduce_scatter | solution.py:73
  522.4 32.3 %reduce-scatter.40.cloned.1.call-done = f32[128,1024]{1,0:T(8,128)} async-done(((f32[512,1024]{1,0:T(8,128)}), f32[128,1024]{1,0:T(8,128)}) %reduce-scatter.40.cloned.1.call-update) | async-done | bytes 524304 | tf_op jit(solution)/shard_map/reduce_scatter | solution.py:73
  557.3 30.9 %reduce-scatter.44.cloned.1.call-done = f32[128,1024]{1,0:T(8,128)} async-done(((f32[512,1024]{1,0:T(8,128)}), f32[128,1024]{1,0:T(8,128)}) %reduce-scatter.44.cloned.1.call-update) | async-done | bytes 524304 | tf_op jit(solution)/shard_map/reduce_scatter | solution.py:73
  590.7 31.3 %reduce-scatter.50.cloned.1.call-done = f32[128,1024]{1,0:T(8,128)} async-done(((f32[512,1024]{1,0:T(8,128)}), f32[128,1024]{1,0:T(8,128)}) %reduce-scatter.50.cloned.1.call-update) | async-done | bytes 524304 | tf_op jit(solution)/shard_map/reduce_scatter | solution.py:73
  625.2 30.4 %reduce-scatter.34.cloned.1.call-done = f32[128,1024]{1,0:T(8,128)} async-done(((f32[512,1024]{1,0:T(8,128)}), f32[128,1024]{1,0:T(8,128)}) %reduce-scatter.34.cloned.1.call-update) | async-done | bytes 524304 | tf_op jit(solution)/shard_map/reduce_scatter | solution.py:73
  658.9 16.8 all-gather.46.cloned.1.call-done
  686.1 31.3 %reduce-scatter.52.cloned.1.call-done = f32[128,1024]{1,0:T(8,128)} async-done(((f32[512,1024]{1,0:T(8,128)}), f32[128,1024]{1,0:T(8,128)}) %reduce-scatter.52.cloned.1.call-update) | async-done | bytes 524304 | tf_op jit(solution)/shard_map/reduce_scatter | solution.py:73
  724.3 15.1 all-gather.62.cloned.1.call-done
  768.1 7.7 all-gather.50.cloned.1.call-done
  787.5 22.5 %reduce-scatter.54.cloned.1.call-done = f32[128,1024]{1,0:T(8,128)} async-done(((f32[512,1024]{1,0:T(8,128)}), f32[128,1024]{1,0:T(8,128)}) %reduce-scatter.54.cloned.1.call-update) | async-done | bytes 524304 | tf_op jit(solution)/shard_map/reduce_scatter | solution.py:73
  813.2 30.4 %reduce-scatter.38.cloned.1.call-done = f32[128,1024]{1,0:T(8,128)} async-done(((f32[512,1024]{1,0:T(8,128)}), f32[128,1024]{1,0:T(8,128)}) %reduce-scatter.38.cloned.1.call-update) | async-done | bytes 524304 | tf_op jit(solution)/shard_map/reduce_scatter | solution.py:73
  843.5 33.7 %reduce-scatter.60.cloned.1.call-done = f32[128,1024]{1,0:T(8,128)} async-done(((f32[512,1024]{1,0:T(8,128)}), f32[128,1024]{1,0:T(8,128)}) %reduce-scatter.60.cloned.1.call-update) | async-done | bytes 524304 | tf_op jit(solution)/shard_map/reduce_scatter | solution.py:73
  877.3 33.7 %reduce-scatter.56.cloned.1.call-done = f32[128,1024]{1,0:T(8,128)} async-done(((f32[512,1024]{1,0:T(8,128)}), f32[128,1024]{1,0:T(8,128)}) %reduce-scatter.56.cloned.1.call-update) | async-done | bytes 524304 | tf_op jit(solution)/shard_map/reduce_scatter | solution.py:73
  918.3 16.1 all-gather.66.cloned.1.call-done
  1020.5 34.3 %reduce-scatter.62.cloned.1.call-done = f32[128,1024]{1,0:T(8,128)} async-done(((f32[512,1024]{1,0:T(8,128)}), f32[128,1024]{1,0:T(8,128)}) %reduce-scatter.62.cloned.1.call-update) | async-done | bytes 524304 | tf_op jit(solution)/shard_map/reduce_scatter | solution.py:73
  1057.9 30.7 %reduce-scatter.46.cloned.1.call-done = f32[128,1024]{1,0:T(8,128)} async-done(((f32[512,1024]{1,0:T(8,128)}), f32[128,1024]{1,0:T(8,128)}) %reduce-scatter.46.cloned.1.call-update) | async-done | bytes 524304 | tf_op jit(solution)/shard_map/reduce_scatter | solution.py:73
  1095.1 12.2 all-gather.60.cloned.1.call-done
  1109.6 16.4 all-gather.44.cloned.1.call-done
  1129.5 65.5 %reduce-scatter.72.cloned.1.call-done = bf16[128,704]{1,0:T(8,128)(2,1)} async-done(((bf16[1024,704]{1,0:T(8,128)(2,1)}), bf16[128,704]{1,0:T(8,128)(2,1)}) %reduce-scatter.72.cloned.1.call-update) | async-done | bytes 180240
  1196.9 65.9 %reduce-scatter.74.cloned.1.call-done = bf16[128,704]{1,0:T(8,128)(2,1)} async-done(((bf16[1024,704]{1,0:T(8,128)(2,1)}), bf16[128,704]{1,0:T(8,128)(2,1)}) %reduce-scatter.74.cloned.1.call-update) | async-done | bytes 180240
  1264.6 65.9 %reduce-scatter.76.cloned.1.call-done = bf16[128,704]{1,0:T(8,128)(2,1)} async-done(((bf16[1024,704]{1,0:T(8,128)(2,1)}), bf16[128,704]{1,0:T(8,128)(2,1)}) %reduce-scatter.76.cloned.1.call-update) | async-done | bytes 180240
  1343.1 4.6 all-gather.64.cloned.1.call-done
  1350.0 16.0 all-gather.48.cloned.1.call-done
  1370.1 61.7 %reduce-scatter.70.cloned.1.call-done = bf16[128,256]{1,0:T(8,128)(2,1)} async-done(((bf16[1024,256]{1,0:T(8,128)(2,1)}), bf16[128,256]{1,0:T(8,128)(2,1)}) %reduce-scatter.70.cloned.1.call-update) | async-done | bytes 65552
  1433.5 63.4 %reduce-scatter.64.cloned.1.call-done = bf16[128,256]{1,0:T(8,128)(2,1)} async-done(((bf16[1024,256]{1,0:T(8,128)(2,1)}), bf16[128,256]{1,0:T(8,128)(2,1)}) %reduce-scatter.64.cloned.1.call-update) | async-done | bytes 65552 | tf_op jit(solution)/shard_map/reduce_scatter | solution.py:294
  1498.3 63.3 %reduce-scatter.66.cloned.1.call-done = bf16[128,256]{1,0:T(8,128)(2,1)} async-done(((bf16[1024,256]{1,0:T(8,128)(2,1)}), bf16[128,256]{1,0:T(8,128)(2,1)}) %reduce-scatter.66.cloned.1.call-update) | async-done | bytes 65552 | tf_op jit(solution)/shard_map/reduce_scatter | solution.py:297
  1563.1 63.3 %reduce-scatter.68.cloned.1.call-done = bf16[128,256]{1,0:T(8,128)(2,1)} async-done(((bf16[1024,256]{1,0:T(8,128)(2,1)}), bf16[128,256]{1,0:T(8,128)(2,1)}) %reduce-scatter.68.cloned.1.call-update) | async-done | bytes 65552 | tf_op jit(solution)/shard_map/reduce_scatter | solution.py:300
  1628.0 40.0 %all-reduce = (f32[1024]{0:T(1024)}, f32[1024]{0:T(1024)}) all-reduce(f32[1024]{0:T(1024)S(1)} %add_add_fusion.5, f32[1024]{0:T(1024)S(1)} %add_add_fusion.4), channel_id=1, replica_groups=mesh['row'=8,'col'=4] {'row','col'}, use_global_device_ids=true, to_apply=%region_64.69 | all-reduce | flops 2048 | bytes 16384 | tf_op jit(solution)/shard_map/psum | solution.py:316
  1672.7 7.4 all-gather.56.cloned.1.call-done
  1682.8 15.6 all-gather.52.cloned.1.call-done
  (952 shorter events, 360.7 us)
Async XLA Ops:
  7.2 150.8 %all-gather.74.cloned.1.call-start = ((), (), s32[]{:S(2)}) async-start(), calls=%async_computation.61 | async-start | bytes 1310720 | tf_op jit(solution)/shard_map/all_gather | solution.py:135
  9.5 153.6 %all-gather.76.cloned.1.call-start = ((), (), s32[]{:S(2)}) async-start(), calls=%async_computation.62 | async-start | bytes 1310720 | tf_op jit(solution)/shard_map/all_gather | solution.py:135
  10.3 158.0 %all-gather.78.cloned.1.call-start = ((), (), s32[]{:S(2)}) async-start(), calls=%async_computation.63 | async-start | bytes 1310720 | tf_op jit(solution)/shard_map/all_gather | solution.py:135
  11.0 163.1 %all-gather.80.cloned.1.call-start = ((), (), s32[]{:S(2)}) async-start(), calls=%async_computation.64 | async-start | bytes 1310720 | tf_op jit(solution)/shard_map/all_gather | solution.py:135
  11.6 180.9 %all-gather.82.cloned.1.call-start = ((), (), s32[]{:S(2)}) async-start(), calls=%async_computation.65 | async-start | bytes 1310720 | tf_op jit(solution)/shard_map/all_gather | solution.py:136
  12.7 209.6 %reduce-scatter.32.cloned.1.call-start = ((), (), s32[]{:S(2)}) async-start(), calls=%async_computation.23 | async-start | bytes 2621440 | tf_op jit(solution)/shard_map/reduce_scatter | solution.py:73
  191.7 75.6 %all-gather.38.cloned.1.call-start = ((), (), s32[]{:S(2)}) async-start(), calls=%async_computation.25 | async-start | bytes 1622016 | tf_op jit(solution)/shard_map/all_gather | solution.py:125
  192.4 91.9 %all-gather.36.cloned.1.call-start = ((), (), s32[]{:S(2)}) async-start(), calls=%async_computation.24 | async-start | bytes 1310720 | tf_op jit(solution)/shard_map/all_gather | solution.py:69
  225.2 104.2 %all-gather.40.cloned.1.call-start = ((), (), s32[]{:S(2)}) async-start(), calls=%async_computation.26 | async-start | bytes 1622016 | tf_op jit(solution)/shard_map/all_gather | solution.py:126
  226.0 146.5 %all-gather.42.cloned.1.call-start = ((), (), s32[]{:S(2)}) async-start(), calls=%async_computation.27 | async-start | bytes 1622016 | tf_op jit(solution)/shard_map/all_gather | solution.py:127
  226.5 184.8 %reduce-scatter.48.cloned.1.call-start = ((), (), s32[]{:S(2)}) async-start(), calls=%async_computation.42 | async-start | bytes 2621440 | tf_op jit(solution)/shard_map/reduce_scatter | solution.py:73
  381.8 76.0 %all-gather.58.cloned.1.call-start = ((), (), s32[]{:S(2)}) async-start(), calls=%async_computation.43 | async-start | bytes 1310720 | tf_op jit(solution)/shard_map/all_gather | solution.py:69
  415.5 62.9 %all-gather.88.cloned.1.call-start = ((), (), s32[]{:S(2)}) async-start(), calls=%async_computation.68 | async-start | bytes 1310720 | tf_op jit(solution)/shard_map/all_gather | solution.py:136
  416.2 67.0 %all-gather.86.cloned.1.call-start = ((), (), s32[]{:S(2)}) async-start(), calls=%async_computation.67 | async-start | bytes 1310720 | tf_op jit(solution)/shard_map/all_gather | solution.py:136
  416.8 71.3 %all-gather.84.cloned.1.call-start = ((), (), s32[]{:S(2)}) async-start(), calls=%async_computation.66 | async-start | bytes 1310720 | tf_op jit(solution)/shard_map/all_gather | solution.py:136
  417.4 103.1 %reduce-scatter.36.cloned.1.call-start = ((), (), s32[]{:S(2)}) async-start(), calls=%async_computation.30 | async-start | bytes 2621440 | tf_op jit(solution)/shard_map/reduce_scatter | solution.py:73
  432.3 122.4 %reduce-scatter.40.cloned.1.call-start = ((), (), s32[]{:S(2)}) async-start(), calls=%async_computation.34 | async-start | bytes 2621440 | tf_op jit(solution)/shard_map/reduce_scatter | solution.py:73
  443.7 144.5 %reduce-scatter.44.cloned.1.call-start = ((), (), s32[]{:S(2)}) async-start(), calls=%async_computation.38 | async-start | bytes 2621440 | tf_op jit(solution)/shard_map/reduce_scatter | solution.py:73
  457.7 164.3 %reduce-scatter.50.cloned.1.call-start = ((), (), s32[]{:S(2)}) async-start(), calls=%async_computation.44 | async-start | bytes 2621440 | tf_op jit(solution)/shard_map/reduce_scatter | solution.py:73
  472.0 183.6 %reduce-scatter.34.cloned.1.call-start = ((), (), s32[]{:S(2)}) async-start(), calls=%async_computation.28 | async-start | bytes 2621440 | tf_op jit(solution)/shard_map/reduce_scatter | solution.py:73
  476.9 198.8 %all-gather.46.cloned.1.call-start = ((), (), s32[]{:S(2)}) async-start(), calls=%async_computation.31 | async-start | bytes 1310720 | tf_op jit(solution)/shard_map/all_gather | solution.py:69
  658.8 58.5 %reduce-scatter.52.cloned.1.call-start = ((), (), s32[]{:S(2)}) async-start(), calls=%async_computation.46 | async-start | bytes 2621440 | tf_op jit(solution)/shard_map/reduce_scatter | solution.py:73
  686.0 53.3 %all-gather.62.cloned.1.call-start = ((), (), s32[]{:S(2)}) async-start(), calls=%async_computation.47 | async-start | bytes 1310720 | tf_op jit(solution)/shard_map/all_gather | solution.py:69
  723.1 52.7 %all-gather.50.cloned.1.call-start = ((), (), s32[]{:S(2)}) async-start(), calls=%async_computation.35 | async-start | bytes 1310720 | tf_op jit(solution)/shard_map/all_gather | solution.py:69
  723.8 86.1 %reduce-scatter.54.cloned.1.call-start = ((), (), s32[]{:S(2)}) async-start(), calls=%async_computation.48 | async-start | bytes 2621440 | tf_op jit(solution)/shard_map/reduce_scatter | solution.py:73
  753.3 90.2 %reduce-scatter.38.cloned.1.call-start = ((), (), s32[]{:S(2)}) async-start(), calls=%async_computation.32 | async-start | bytes 2621440 | tf_op jit(solution)/shard_map/reduce_scatter | solution.py:73
  757.4 119.9 %reduce-scatter.60.cloned.1.call-start = ((), (), s32[]{:S(2)}) async-start(), calls=%async_computation.54 | async-start | bytes 2621440 | tf_op jit(solution)/shard_map/reduce_scatter | solution.py:73
  767.9 143.1 %reduce-scatter.56.cloned.1.call-start = ((), (), s32[]{:S(2)}) async-start(), calls=%async_computation.50 | async-start | bytes 2621440 | tf_op jit(solution)/shard_map/reduce_scatter | solution.py:73
  786.2 148.2 %all-gather.66.cloned.1.call-start = ((), (), s32[]{:S(2)}) async-start(), calls=%async_computation.51 | async-start | bytes 1310720 | tf_op jit(solution)/shard_map/all_gather | solution.py:69
  918.2 97.0 %reduce-scatter.58.cloned.1.call-start = ((), (), s32[]{:S(2)}) async-start(), calls=%async_computation.52 | async-start | bytes 2621440 | tf_op jit(solution)/shard_map/reduce_scatter | solution.py:73
  948.5 72.0 %reduce-scatter.42.cloned.1.call-start = ((), (), s32[]{:S(2)}) async-start(), calls=%async_computation.36 | async-start | bytes 2621440 | tf_op jit(solution)/shard_map/reduce_scatter | solution.py:73
  953.3 101.6 %reduce-scatter.62.cloned.1.call-start = ((), (), s32[]{:S(2)}) async-start(), calls=%async_computation.56 | async-start | bytes 2621440 | tf_op jit(solution)/shard_map/reduce_scatter | solution.py:73
  966.7 121.9 %reduce-scatter.46.cloned.1.call-start = ((), (), s32[]{:S(2)}) async-start(), calls=%async_computation.40 | async-start | bytes 2621440 | tf_op jit(solution)/shard_map/reduce_scatter | solution.py:73
  971.6 135.7 %all-gather.60.cloned.1.call-start = ((), (), s32[]{:S(2)}) async-start(), calls=%async_computation.45 | async-start | bytes 1310720 | tf_op jit(solution)/shard_map/all_gather | solution.py:284
  972.2 153.9 %all-gather.44.cloned.1.call-start = ((), (), s32[]{:S(2)}) async-start(), calls=%async_computation.29 | async-start | bytes 1310720 | tf_op jit(solution)/shard_map/all_gather | solution.py:281
  972.8 222.3 %reduce-scatter.72.cloned.1.call-start = ((), (), s32[]{:S(2)}) async-start(), calls=%async_computation.70 | async-start | bytes 1769472
  979.7 283.1 %reduce-scatter.74.cloned.1.call-start = ((), (), s32[]{:S(2)}) async-start(), calls=%async_computation.71 | async-start | bytes 1769472
  987.3 343.3 %reduce-scatter.76.cloned.1.call-start = ((), (), s32[]{:S(2)}) async-start(), calls=%async_computation.72 | async-start | bytes 1769472
  994.2 353.5 %all-gather.64.cloned.1.call-start = ((), (), s32[]{:S(2)}) async-start(), calls=%async_computation.49 | async-start | bytes 1310720 | tf_op jit(solution)/shard_map/all_gather | solution.py:284
  995.0 371.0 %all-gather.48.cloned.1.call-start = ((), (), s32[]{:S(2)}) async-start(), calls=%async_computation.33 | async-start | bytes 1310720 | tf_op jit(solution)/shard_map/all_gather | solution.py:281
  995.7 436.1 %reduce-scatter.70.cloned.1.call-start = ((), (), s32[]{:S(2)}) async-start(), calls=%async_computation.69 | async-start | bytes 589824
  1000.7 496.1 %reduce-scatter.64.cloned.1.call-start = ((), (), s32[]{:S(2)}) async-start(), calls=%async_computation.58 | async-start | bytes 589824 | tf_op jit(solution)/shard_map/reduce_scatter | solution.py:294
  1005.1 556.5 %reduce-scatter.66.cloned.1.call-start = ((), (), s32[]{:S(2)}) async-start(), calls=%async_computation.59 | async-start | bytes 589824 | tf_op jit(solution)/shard_map/reduce_scatter | solution.py:297
  1009.7 616.8 %reduce-scatter.68.cloned.1.call-start = ((), (), s32[]{:S(2)}) async-start(), calls=%async_computation.60 | async-start | bytes 589824 | tf_op jit(solution)/shard_map/reduce_scatter | solution.py:300
  1015.1 652.9 %all-gather.72.cloned.1.call-start = ((), (), s32[]{:S(2)}) async-start(), calls=%async_computation.57 | async-start | bytes 1310720 | tf_op jit(solution)/shard_map/all_gather | solution.py:284
  1091.0 579.3 %all-gather.68.cloned.1.call-start = ((), (), s32[]{:S(2)}) async-start(), calls=%async_computation.53 | async-start | bytes 1310720 | tf_op jit(solution)/shard_map/all_gather | solution.py:284
  1091.6 588.6 %all-gather.56.cloned.1.call-start = ((), (), s32[]{:S(2)}) async-start(), calls=%async_computation.41 | async-start | bytes 1310720 | tf_op jit(solution)/shard_map/all_gather | solution.py:281
  1092.1 606.3 %all-gather.52.cloned.1.call-start = ((), (), s32[]{:S(2)}) async-start(), calls=%async_computation.37 | async-start | bytes 1310720 | tf_op jit(solution)/shard_map/all_gather | solution.py:281
  (267 other events, 4432.5 us)
Sparse Core Ops, SparseCore 0:
  10.1 19.4 all-gather.73
  31.7 16.6 all-gather.75
  50.6 16.6 all-gather.77
  69.3 16.6 all-gather.79
  88.0 16.6 all-gather.81
  191.8 30.3 reduce-scatter.31
  224.3 42.9 all-gather.37
  286.4 42.9 all-gather.39
  331.3 41.1 all-gather.41
  381.9 29.3 reduce-scatter.47
  415.6 16.6 all-gather.57
  433.9 16.6 all-gather.87
  452.1 16.6 all-gather.85
  470.2 16.6 all-gather.83
  489.3 31.1 reduce-scatter.35
  523.5 31.1 reduce-scatter.39
  557.1 31.1 reduce-scatter.43
  590.8 31.1 reduce-scatter.49
  624.4 31.1 reduce-scatter.33
  659.0 16.6 all-gather.45
  686.1 31.1 reduce-scatter.51
  722.6 16.6 all-gather.61
  740.7 16.7 all-gather.53
  759.1 16.6 all-gather.49
  778.7 31.1 reduce-scatter.53
  812.3 31.1 reduce-scatter.37
  846.0 31.1 reduce-scatter.59
  879.8 31.1 reduce-scatter.55
  917.6 16.6 all-gather.65
  936.5 16.6 all-gather.69
  955.7 31.1 reduce-scatter.57
  989.3 31.1 reduce-scatter.41
  1023.6 31.1 reduce-scatter.61
  1057.4 31.1 reduce-scatter.45
  1090.6 16.6 all-gather.59
  1109.3 16.6 all-gather.43
  1129.4 65.5 reduce-scatter.71
  1198.3 64.4 reduce-scatter.73
  1266.2 64.3 reduce-scatter.75
  1349.3 16.6 all-gather.47
  1369.2 62.6 reduce-scatter.69
  1435.2 61.6 reduce-scatter.63
  1500.0 61.5 reduce-scatter.65
  1564.8 61.5 reduce-scatter.67
  1627.9 15.7 all-gather.71
  1645.1 16.9 all-gather.67
  1663.5 16.6 all-gather.55
  1681.7 16.6 all-gather.51
  (2 shorter events, 30.3 us)
where the time goes:
time: 1720 us; the launch traced here: 1710 us
  waiting for transfers between devices  1140 us (66%)
  blocking collectives  166 us (10%)
  matrix products  148 us (9%)
  local copies, waits for them, and re-layouts  131 us (8%)
  other arithmetic  99.4 us (6%)
  between operations  18.5 us (1%)
    reduce_scatter x16, waiting for transfers between devices, reduce_tokens(): return lax.psum_scatter(values, 'col', scatter_dimension=0, tiled=True)  417 us
    unnamed x54, waiting for transfers between devices  270 us
    all_gather x8, waiting for transfers between devices, spread_tokens(): return lax.all_gather(values, 'col', axis=0, tiled=True)  72.8 us
    reduce_scatter x1, waiting for transfers between devices, body(): lax.psum_scatter(grads_full[0].astype(jnp.bfloat16), 'row', scatter_dimen...  63.4 us
    reduce_scatter x1, waiting for transfers between devices, body(): lax.psum_scatter(grads_full[1].astype(jnp.bfloat16), 'row', scatter_dimen...  63.3 us
    reduce_scatter x1, waiting for transfers between devices, body(): lax.psum_scatter(grads_full[2].astype(jnp.bfloat16), 'row', scatter_dimen...  63.3 us
    all_gather x4, waiting for transfers between devices, body(): lax.all_gather(packed_out.astype(jnp.float32).astype(jnp.bfloat16), 'col'...  55.5 us
    dot_general x28, matrix products, product(): return jnp.dot(left, right, preferred_element_type=jnp.float32)  46.7 us
  transfers between devices with their start and end apart: 50, of which 37 were waited for; matrix products, arithmetic and copies ran while one was open for 18% of the time, Pallas kernels for 0%

commit v1 on v0

--- a/solution.py
+++ b/solution.py
@@ -73,7 +73,7 @@
     return lax.psum_scatter(values, "col", scatter_dimension=0, tiled=True)
 
 
-def body(
+def tiled_body(
     hidden_in,
     first_values,
     lengths,
@@ -330,7 +330,210 @@
     )
 
 
+def slot_body(
+    hidden_in,
+    first_values,
+    lengths,
+    places,
+    gain_attn,
+    gain_ffn,
+    w_query,
+    w_key,
+    w_value,
+    w_out,
+    w_gate,
+    w_up,
+    w_down,
+    out_grad,
+):
+    slots, rows, width = hidden_in.shape
+    count = slots * rows
+    heads = width // HEAD_DIM
+    hidden_tile = w_gate.shape[1]
+    column = lax.axis_index("col")
+    score_scale = HEAD_DIM ** (-0.5)
+    both = ("row", "col")
+
+    def gather(tile):
+        return lax.all_gather(tile, both, axis=0, tiled=False)
+
+    row_count = width // w_query.shape[0]
+
+    def by_rows(whole, count_out):
+        tile_rows, tile_cols = whole.shape[1:]
+        whole = whole.reshape(row_count, slots, tile_rows, tile_cols)
+        return jnp.transpose(whole, (0, 2, 1, 3)).reshape(row_count * tile_rows, count_out)
+
+    def by_cols(whole, count_in):
+        tile_rows, tile_cols = whole.shape[1:]
+        whole = whole.reshape(row_count, slots, tile_rows, tile_cols)
+        return jnp.transpose(whole, (1, 2, 0, 3)).reshape(count_in, row_count * tile_cols)
+
+    ff = hidden_tile * slots
+    wide = w_query.shape[1]
+    qkv_tiles = gather(jnp.concatenate([w_query, w_key, w_value], axis=1))
+    wq = by_rows(qkv_tiles[:, :, :wide], width)
+    wk = by_rows(qkv_tiles[:, :, wide : 2 * wide], width)
+    wv = by_rows(qkv_tiles[:, :, 2 * wide :], width)
+    wo = by_cols(gather(w_out), width)
+    wg = by_rows(gather(w_gate), ff)
+    wu = by_rows(gather(w_up), ff)
+    wd = by_cols(gather(w_down), ff)
+
+    first_rows = jnp.transpose(first_values, (0, 2, 1))
+    feature_tile = first_rows.shape[2]
+    first_packed = first_rows.reshape(slots, slots, rows, feature_tile)
+    first_packed = jnp.transpose(first_packed, (0, 2, 1, 3)).reshape(slots, rows, width)
+    sent = jnp.concatenate([hidden_in, out_grad, first_packed], axis=1)
+    got = lax.all_to_all(sent, "col", split_axis=0, concat_axis=0, tiled=True)
+    hidden = got[:, :rows].reshape(count, width).astype(jnp.float32)
+    grad_rows = got[:, rows : 2 * rows].reshape(count, width)
+    first = got[:, 2 * rows :].reshape(slots, rows, slots, feature_tile)
+    first = jnp.transpose(first, (2, 1, 0, 3)).reshape(count, width).astype(jnp.float32)
+
+    place = lax.dynamic_index_in_dim(places, column, 0, keepdims=False)
+    length = lax.dynamic_index_in_dim(lengths, column, 0, keepdims=False)
+    ends_at = jnp.cumsum(length)
+    starts_at = ends_at - length
+    past = place[:, None] >= ends_at[None, :]
+    segment_id = jnp.sum(past.astype(jnp.int32), axis=1)
+    one_hot = segment_id[:, None] == jnp.arange(length.shape[0], dtype=jnp.int32)[None, :]
+    position = place - jnp.sum(jnp.where(one_hot, starts_at[None, :], 0), axis=1)
+    cosine, sine = rotary_tables(position)
+    allowed = (segment_id[:, None] == segment_id[None, :]) & (place[:, None] >= place[None, :])
+
+    scale_one = lax.rsqrt(jnp.mean(hidden * hidden, axis=1, keepdims=True) + EPSILON)
+    normed_one = (hidden * scale_one * gain_attn).astype(jnp.bfloat16)
+    by_head = (count, heads, HEAD_DIM)
+    queries = rotate(product(normed_one, wq).reshape(by_head), cosine, sine).astype(jnp.bfloat16)
+    keys = rotate(product(normed_one, wk).reshape(by_head), cosine, sine).astype(jnp.bfloat16)
+    values = (0.5 * product(normed_one, wv) + 0.5 * first).astype(jnp.bfloat16).reshape(by_head)
+
+    raw_scores = jnp.einsum("qhd,khd->hqk", queries, keys, preferred_element_type=jnp.float32)
+    scores = jnp.where(allowed[None], raw_scores * score_scale, MASKED)
+    row_top = jnp.max(scores, axis=-1, keepdims=True)
+    log_total = row_top + jnp.log(jnp.sum(jnp.exp(scores - row_top), axis=-1, keepdims=True))
+    probs = jnp.exp(scores - log_total)
+    probs_low = probs.astype(jnp.bfloat16)
+    attended = (
+        jnp.einsum("hqk,khd->qhd", probs_low, values, preferred_element_type=jnp.float32)
+        .astype(jnp.bfloat16)
+        .reshape(count, width)
+    )
+    mid = hidden + product(attended, wo)
+    scale_two = lax.rsqrt(jnp.mean(mid * mid, axis=1, keepdims=True) + EPSILON)
+    normed_two = (mid * scale_two * gain_ffn).astype(jnp.bfloat16)
+    gate_raw = product(normed_two, wg)
+    up_raw = product(normed_two, wu)
+    sigmoid_gate = jax.nn.sigmoid(gate_raw)
+    silu_gate = gate_raw * sigmoid_gate
+    hidden_act = (silu_gate * up_raw).astype(jnp.bfloat16)
+    stored_out = (mid + product(hidden_act, wd)).astype(jnp.bfloat16)
+
+    def scatter(tiles):
+        tiles = tiles.reshape((row_count * slots,) + tiles.shape[2:])
+        return lax.psum_scatter(tiles, both, scatter_dimension=0, tiled=False).astype(jnp.float32)
+
+    def tiles_by_rows(grad):
+        depth, across = grad.shape
+        grad = grad.astype(jnp.bfloat16)
+        grad = grad.reshape(row_count, depth // row_count, slots, across // slots)
+        return scatter(jnp.transpose(grad, (0, 2, 1, 3)))
+
+    def tiles_by_cols(grad):
+        depth, across = grad.shape
+        grad = grad.astype(jnp.bfloat16)
+        grad = grad.reshape(slots, depth // slots, row_count, across // row_count)
+        return scatter(jnp.transpose(grad, (2, 0, 1, 3)))
+
+    grad_down = tiles_by_cols(product_left(hidden_act, grad_rows))
+    d_hidden = product_right(grad_rows, wd)
+    d_gate = (d_hidden * up_raw * sigmoid_gate * (1.0 + gate_raw * (1.0 - sigmoid_gate))).astype(
+        jnp.bfloat16
+    )
+    d_up = (d_hidden * silu_gate).astype(jnp.bfloat16)
+    grad_gate = tiles_by_rows(product_left(normed_two, d_gate))
+    grad_up = tiles_by_rows(product_left(normed_two, d_up))
+    d_normed_two = product_right(d_gate, wg) + product_right(d_up, wu)
+    gain_sum_two = jnp.sum(d_normed_two * mid * scale_two, axis=0)
+    scaled_two = d_normed_two * gain_ffn
+    stat_two = jnp.sum(scaled_two * mid, axis=1, keepdims=True)
+    d_mid = (
+        grad_rows.astype(jnp.float32)
+        + scale_two * scaled_two
+        - mid * (scale_two * scale_two * scale_two * stat_two / width)
+    )
+    d_branch = d_mid.astype(jnp.bfloat16)
+    grad_out = tiles_by_cols(product_left(attended, d_branch))
+    d_attended = product_right(d_branch, wo).astype(jnp.bfloat16).reshape(by_head)
+    d_probs = jnp.einsum("qhd,khd->hqk", d_attended, values, preferred_element_type=jnp.float32)
+    inner_sum = jnp.sum(probs * d_probs, axis=-1, keepdims=True)
+    d_scores = (probs * (d_probs - inner_sum)).astype(jnp.bfloat16)
+    d_query = score_scale * jnp.einsum(
+        "hqk,khd->qhd", d_scores, keys, preferred_element_type=jnp.float32
+    )
+    d_key = score_scale * jnp.einsum(
+        "hqk,qhd->khd", d_scores, queries, preferred_element_type=jnp.float32
+    )
+    d_values = (
+        jnp.einsum("hqk,qhd->khd", probs_low, d_attended, preferred_element_type=jnp.float32)
+        .astype(jnp.bfloat16)
+        .reshape(count, width)
+    )
+    d_value_proj = (0.5 * d_values.astype(jnp.float32)).astype(jnp.bfloat16)
+    d_query_raw = rotate_back(d_query, cosine, sine).astype(jnp.bfloat16).reshape(count, width)
+    d_key_raw = rotate_back(d_key, cosine, sine).astype(jnp.bfloat16).reshape(count, width)
+    grad_query = tiles_by_rows(product_left(normed_one, d_query_raw))
+    grad_key = tiles_by_rows(product_left(normed_one, d_key_raw))
+    grad_value = tiles_by_rows(product_left(normed_one, d_value_proj))
+    d_normed_one = (
+        product_right(d_query_raw, wq)
+        + product_right(d_key_raw, wk)
+        + product_right(d_value_proj, wv)
+    )
+    gain_sum_one = jnp.sum(d_normed_one * hidden * scale_one, axis=0)
+    scaled_one = d_normed_one * gain_attn
+    stat_one = jnp.sum(scaled_one * hidden, axis=1, keepdims=True)
+    input_grad = (
+        d_mid
+        + scale_one * scaled_one
+        - hidden * (scale_one * scale_one * scale_one * stat_one / width)
+    )
+    value_sent = d_value_proj.reshape(slots, rows, slots, feature_tile)
+    value_sent = jnp.transpose(value_sent, (2, 1, 0, 3)).reshape(slots, rows, width)
+    sent_back = jnp.concatenate(
+        [
+            stored_out.reshape(slots, rows, width),
+            input_grad.astype(jnp.bfloat16).reshape(slots, rows, width),
+            value_sent,
+        ],
+        axis=1,
+    )
+    back = lax.all_to_all(sent_back, "col", split_axis=0, concat_axis=0, tiled=True)
+    value_back = back[:, 2 * rows :].reshape(slots, rows, slots, feature_tile)
+    value_back = jnp.transpose(value_back, (0, 3, 2, 1)).reshape(slots, feature_tile, count)
+    gain_grad_one, gain_grad_two = lax.psum((gain_sum_one, gain_sum_two), both)
+    return (
+        back[:, :rows],
+        back[:, rows : 2 * rows].astype(jnp.float32),
+        value_back.astype(jnp.float32),
+        gain_grad_one,
+        gain_grad_two,
+        grad_query,
+        grad_key,
+        grad_value,
+        grad_out,
+        grad_gate,
+        grad_up,
+        grad_down,
+    )
+
+
 def solution(mesh):
+    def body(*arrays):
+        one_each = arrays[0].shape[0] == mesh.shape["col"]
+        return (slot_body if one_each else tiled_body)(*arrays)
+
     return jax.shard_map(
         body,
         mesh=mesh,

time: 1720 us -> 1450 us (0.84)
  waiting for transfers between devices: 1140 us -> 993 us
  blocking collectives: 166 us -> 78 us
  other arithmetic: 99.4 us -> 53.2 us
  local copies, waits for them, and re-layouts: 131 us -> 169 us
  matrix products: 148 us -> 124 us
    unnamed x54 -> x12, waiting for transfers between devices: 270 us -> 2.71 us
    all_gather x4 -> x0, blocking collectives: 126 us -> none  [the longest x1 33.4 us: body(): lax.all_gather(tiles[2], 'row', axis=0, tiled=True)]
    reduce_scatter x19 -> x7, waiting for transfers between devices: 607 us -> 712 us  [scatter(): lax.psum_scatter(tiles, both, scatter_dimension=0, tiled=False)]
    reshape x1 -> x16, local copies, waits for them, and re-layouts: 0.01 us -> 85 us  [the longest x5 38 us: tiles_by_rows(): grad = grad.reshape(row_count, depth // row_count, slots, across // slots)]
    gather x28 -> x0, local copies, waits for them, and re-layouts: 69.5 us -> none  [the longest x4 19.4 us: body(): grad_full_rows = jnp.take(stored_grad, packed_order, axis=0)]
    transpose x0 -> x13, local copies, waits for them, and re-layouts: none -> 41.7 us  [the longest x5 26.3 us: tiles_by_rows(): return scatter(jnp.transpose(grad, (0, 2, 1, 3)))]
    all_to_all x0 -> x2, waiting for transfers between devices: none -> 40.9 us  [the longest x1 40.9 us: slot_body(): got = lax.all_to_all(sent, 'col', split_axis=0, concat_axis=0, tiled=True)]
    psum x1, blocking collectives: 40 us -> 78 us  [slot_body(): gain_grad_one, gain_grad_two = lax.psum((gain_sum_one, gain_sum_two), both)]
  transfers between devices with their start and end apart: 50 -> 14, of which waited for: 37 -> 11; matrix products, arithmetic and copies ran while one was open for 18% -> 17% of each run, Pallas kernels for 0% -> 0%
where the time goes in v1:
time: 1450 us; the launch traced here: 1440 us
  waiting for transfers between devices  993 us (68%)
  local copies, waits for them, and re-layouts  169 us (12%)
  matrix products  124 us (9%)
  blocking collectives  78 us (5%)
  other arithmetic  53.2 us (4%)
  between operations  15.4 us (1%)
    reduce_scatter x7, waiting for transfers between devices, scatter(): lax.psum_scatter(tiles, both, scatter_dimension=0, tiled=False)  712 us
    all_gather x5, waiting for transfers between devices, gather(): return lax.all_gather(tile, both, axis=0, tiled=False)  238 us
    psum x1, blocking collectives, slot_body(): gain_grad_one, gain_grad_two = lax.psum((gain_sum_one, gain_sum_two), both)  78 us
    all_to_all x1, waiting for transfers between devices, slot_body(): got = lax.all_to_all(sent, 'col', split_axis=0, concat_axis=0, tiled=True)  40.9 us
    reshape x5, local copies, waits for them, and re-layouts, tiles_by_rows(): grad = grad.reshape(row_count, depth // row_count, slots, across // slots)  38 us
    reshape x4, local copies, waits for them, and re-layouts, by_rows(): whole = whole.reshape(row_count, slots, tile_rows, tile_cols)  32.4 us
    dot_general x7, matrix products, product_left(): lax.dot_general(left, right, (((0,), (0,)), ((), ())), preferred_element_...  29.9 us
    dot_general x7, matrix products, product(): return jnp.dot(left, right, preferred_element_type=jnp.float32)  29.5 us
  transfers between devices with their start and end apart: 14, of which 11 were waited for; matrix products, arithmetic and copies ran while one was open for 17% of the time, Pallas kernels for 0%

profile of v1, /device:TPU:0, one launch (start us, length us, event | category | flops | bytes accessed | tf_op | source)
XLA Modules:
  0.0 1441.3 jit_solution(5447310958750242446)
XLA Ops:
  17.7 4.4 all-to-all-start
  23.1 40.9 %all-to-all-done = bf16[4,384,1024]{2,1,0:T(8,128)(2,1)S(1)} async-done(((bf16[4,384,1024]{2,1,0:T(8,128)(2,1)}), bf16[4,384,1024]{2,1,0:T(8,128)(2,1)S(1)}, u32[]{:S(2)}, u32[]{:S(2)}) %all-to-all-start) | async-done | bytes 3145760 | tf_op jit(solution)/shard_map/all_to_all | solution.py:388
  66.6 3.2 reshape.506
  76.7 4.3 copy.103
  81.0 68.7 %all-gather.15.cloned.1.call-done = bf16[4096,704]{0,1:T(8,128)(2,1)} async-done(((bf16[128,704]{0,1:T(8,128)(2,1)}), bf16[4096,704]{0,1:T(8,128)(2,1)}) %all-gather.15.cloned.1.call-update) | async-done | bytes 5767184 | tf_op jit(solution)/shard_map/all_gather | solution.py:358
  149.7 10.3 reshape.471
  160.1 5.9 copy.104
  165.9 60.1 %all-gather.17.cloned.1.call-done = bf16[4096,704]{0,1:T(8,128)(2,1)} async-done(((bf16[128,704]{0,1:T(8,128)(2,1)}), bf16[4096,704]{0,1:T(8,128)(2,1)}) %all-gather.17.cloned.1.call-update) | async-done | bytes 5767184 | tf_op jit(solution)/shard_map/all_gather | solution.py:358
  226.0 10.3 reshape.473
  236.3 5.8 copy.105
  242.2 52.0 %all-gather.19.cloned.1.call-done = bf16[22528,128]{1,0:T(8,128)(2,1)} async-done(((bf16[704,128]{1,0:T(8,128)(2,1)}), bf16[22528,128]{1,0:T(8,128)(2,1)}) %all-gather.19.cloned.1.call-update) | async-done | bytes 5767184 | tf_op jit(solution)/shard_map/all_gather | solution.py:358
  294.2 6.4 copy.106
  303.1 5.1 fusion.2
  308.3 57.2 %all-gather.11.cloned.1.call-done = bf16[4096,768]{1,0:T(8,128)(2,1)} async-done(((bf16[128,768]{1,0:T(8,128)(2,1)}), bf16[4096,768]{1,0:T(8,128)(2,1)}) %all-gather.11.cloned.1.call-update) | async-done | bytes 6291472 | tf_op jit(solution)/shard_map/all_gather | solution.py:358
  365.5 5.6 fusion.73
  387.6 4.5 multiply_convert_fusion.6
  396.4 7.7 fusion
  404.1 9.4 exponential_reduce_fusion
  413.6 8.3 convolution_convert_fusion.6
  425.3 5.0 fusion.12
  430.3 10.3 multiply_convert_fusion.3
  440.6 6.0 fusion.6
  446.6 3.5 multiply_reduce_fusion.1
  454.6 3.8 fusion.48
  460.2 8.4 multiply_convert_fusion.4
  472.2 3.3 reshape.486
  477.3 11.8 multiply_reduce_fusion
  489.2 12.6 multiply_convert_fusion
  511.4 3.3 reshape.482
  516.6 3.9 convolution_convert_fusion.3
  520.5 3.3 reshape.484
  525.6 5.7 convert_bitcast_fusion
  533.2 3.8 copy.121
  538.3 6.8 convolution_convert_fusion.1
  545.1 14.0 reshape.518
  559.1 10.5 copy.127
  569.7 7.0 convolution_convert_fusion
  576.7 14.0 reshape.519
  590.7 10.5 copy.129
  614.6 3.1 add_convert_fusion
  619.6 3.7 all-to-all-start.1
  623.3 78.0 %all-reduce = (f32[1024]{0:T(1024)}, f32[1024]{0:T(1024)}) all-reduce(f32[1024]{0:T(1024)S(1)} %get-tuple-element.12, f32[1024]{0:T(1024)S(1)} %get-tuple-element.14), channel_id=1, replica_groups=mesh['row'=8,'col'=4] {'row','col'}, use_global_device_ids=true, to_apply=%region_11.12 | all-reduce | flops 2048 | bytes 16384 | tf_op jit(solution)/shard_map/psum | solution.py:515
  713.0 15.8 %reduce-scatter.12.cloned.1.call-done = bf16[1,128,256]{2,1,0:T(8,128)(2,1)} async-done(((bf16[32,128,256]{2,1,0:T(8,128)(2,1)}), bf16[1,128,256]{2,1,0:T(8,128)(2,1)}) %reduce-scatter.12.cloned.1.call-update) | async-done | bytes 65552 | tf_op jit(solution)/shard_map/reduce_scatter | solution.py:435
  730.4 134.6 %reduce-scatter.8.cloned.1.call-done = bf16[1,128,256]{2,1,0:T(8,128)(2,1)} async-done(((bf16[32,128,256]{2,1,0:T(8,128)(2,1)}), bf16[1,128,256]{2,1,0:T(8,128)(2,1)}) %reduce-scatter.8.cloned.1.call-update) | async-done | bytes 65552 | tf_op jit(solution)/shard_map/reduce_scatter | solution.py:435
  866.5 134.6 %reduce-scatter.10.cloned.1.call-done = bf16[1,128,256]{2,1,0:T(8,128)(2,1)} async-done(((bf16[32,128,256]{2,1,0:T(8,128)(2,1)}), bf16[1,128,256]{2,1,0:T(8,128)(2,1)}) %reduce-scatter.10.cloned.1.call-update) | async-done | bytes 65552 | tf_op jit(solution)/shard_map/reduce_scatter | solution.py:435
  1002.6 142.3 %reduce-scatter.20.cloned.1.call-done = bf16[1,704,128]{2,1,0:T(8,128)(2,1)} async-done(((bf16[32,704,128]{2,1,0:T(8,128)(2,1)}), bf16[1,704,128]{2,1,0:T(8,128)(2,1)}) %reduce-scatter.20.cloned.1.call-update) | async-done | bytes 180240 | tf_op jit(solution)/shard_map/reduce_scatter | solution.py:435
  1146.6 142.2 %reduce-scatter.16.cloned.1.call-done = bf16[1,128,704]{1,2,0:T(8,128)(2,1)} async-done(((bf16[32,128,704]{1,2,0:T(8,128)(2,1)}), bf16[1,128,704]{1,2,0:T(8,128)(2,1)}) %reduce-scatter.16.cloned.1.call-update) | async-done | bytes 180240 | tf_op jit(solution)/shard_map/reduce_scatter | solution.py:435
  1290.5 142.0 %reduce-scatter.18.cloned.1.call-done = bf16[1,128,704]{1,2,0:T(8,128)(2,1)} async-done(((bf16[32,128,704]{1,2,0:T(8,128)(2,1)}), bf16[1,128,704]{1,2,0:T(8,128)(2,1)}) %reduce-scatter.18.cloned.1.call-update) | async-done | bytes 180240 | tf_op jit(solution)/shard_map/reduce_scatter | solution.py:435
  (220 shorter events, 111.6 us)
Async XLA Ops:
  7.2 15.2 %copy-start = (s32[4,512]{1,0:T(4,128)S(1)}, s32[4,512]{1,0:T(4,128)}, u32[]{:S(2)}) copy-start(s32[4,512]{1,0:T(4,128)} %param.17) | copy-start | bytes 24580
  7.2 69.5 %all-gather.13.cloned.1.call-start = ((), (), s32[]{:S(2)}) async-start(), calls=%async_computation.17 | async-start | bytes 2162688 | tf_op jit(solution)/shard_map/all_gather | solution.py:358
  7.9 141.8 %all-gather.15.cloned.1.call-start = ((), (), s32[]{:S(2)}) async-start(), calls=%async_computation.18 | async-start | bytes 5947392 | tf_op jit(solution)/shard_map/all_gather | solution.py:358
  8.7 217.3 %all-gather.17.cloned.1.call-start = ((), (), s32[]{:S(2)}) async-start(), calls=%async_computation.19 | async-start | bytes 5947392 | tf_op jit(solution)/shard_map/all_gather | solution.py:358
  9.4 284.8 %all-gather.19.cloned.1.call-start = ((), (), s32[]{:S(2)}) async-start(), calls=%async_computation.20 | async-start | bytes 5947392 | tf_op jit(solution)/shard_map/all_gather | solution.py:358
  10.0 355.5 %all-gather.11.cloned.1.call-start = ((), (), s32[]{:S(2)}) async-start(), calls=%async_computation.16 | async-start | bytes 6488064 | tf_op jit(solution)/shard_map/all_gather | solution.py:358
  11.7 3.2 copy-start.37
  17.7 4.4 copy-start.50
  17.7 46.3 %all-to-all-start = ((bf16[4,384,1024]{2,1,0:T(8,128)(2,1)}), bf16[4,384,1024]{2,1,0:T(8,128)(2,1)S(1)}, u32[]{:S(2)}, u32[]{:S(2)}) async-start(bf16[4,384,1024]{2,1,0:T(8,128)(2,1)} %pad_maximum_fusion), calls=%async_computation | async-start | bytes 6291456 | tf_op jit(solution)/shard_map/all_to_all | solution.py:388
  22.1 689.4 %reduce-scatter.14.cloned.1.call-start = ((), (), s32[]{:S(2)}) async-start(), calls=%async_computation.12 | async-start | bytes 2162688 | tf_op jit(solution)/shard_map/reduce_scatter | solution.py:435
  64.0 11.4 copy-start.2
  74.8 6.2 copy-start.44
  294.2 8.9 copy-start.16
  376.8 3.0 copy-start.4
  396.3 7.8 copy-start.20
  396.3 7.8 copy-start.22
  396.4 7.8 copy-start.24
  396.4 7.8 copy-start.26
  413.6 8.3 copy-start.41
  413.6 8.3 copy-start.28
  413.6 8.3 copy-start.29
  421.9 3.4 slice-start.3
  423.3 26.8 %copy-start.8 = (f32[512,1024]{1,0:T(8,128)}, f32[512,1024]{1,0:T(8,128)S(1)}, u32[]{:S(2)}) copy-start(f32[512,1024]{1,0:T(8,128)S(1)} %get-tuple-element.49) | copy-start | bytes 6291460
  423.3 7.0 slice-start.4
  423.6 6.7 copy-start.33
  425.3 5.0 slice-start.5
  440.6 6.0 copy-start.51
  446.6 3.6 copy-start.17
  450.7 3.9 copy-start.10
  454.6 274.3 %reduce-scatter.12.cloned.1.call-start = ((), (), s32[]{:S(2)}) async-start(), calls=%async_computation.11 | async-start | bytes 2162688 | tf_op jit(solution)/shard_map/reduce_scatter | solution.py:435
  460.1 8.5 copy-start.14
  460.2 9.4 copy-start.31
  477.3 11.9 copy-start.43
  489.1 375.9 %reduce-scatter.8.cloned.1.call-start = ((), (), s32[]{:S(2)}) async-start(), calls=%async_computation.9 | async-start | bytes 2162688 | tf_op jit(solution)/shard_map/reduce_scatter | solution.py:435
  489.2 12.6 copy-start.25
  489.2 12.6 copy-start.27
  516.6 484.5 %reduce-scatter.10.cloned.1.call-start = ((), (), s32[]{:S(2)}) async-start(), calls=%async_computation.10 | async-start | bytes 2162688 | tf_op jit(solution)/shard_map/reduce_scatter | solution.py:435
  525.6 619.3 %reduce-scatter.20.cloned.1.call-start = ((), (), s32[]{:S(2)}) async-start(), calls=%async_computation.15 | async-start | bytes 5947392 | tf_op jit(solution)/shard_map/reduce_scatter | solution.py:435
  537.1 751.8 %reduce-scatter.16.cloned.1.call-start = ((), (), s32[]{:S(2)}) async-start(), calls=%async_computation.13 | async-start | bytes 5947392 | tf_op jit(solution)/shard_map/reduce_scatter | solution.py:435
  569.6 862.9 %reduce-scatter.18.cloned.1.call-start = ((), (), s32[]{:S(2)}) async-start(), calls=%async_computation.14 | async-start | bytes 5947392 | tf_op jit(solution)/shard_map/reduce_scatter | solution.py:435
  604.5 3.1 copy-start.7
  604.5 3.1 copy-start.40
  604.5 4.4 copy-start.38
  604.5 4.4 copy-start.48
  604.5 4.4 copy-start.49
  607.6 5.0 slice-start
  619.6 81.7 %all-to-all-start.1 = ((bf16[4,384,1024]{2,1,0:T(8,128)(2,1)}), bf16[4,384,1024]{2,1,0:T(8,128)(2,1)S(1)}, u32[]{:S(2)}, u32[]{:S(2)}) async-start(bf16[4,384,1024]{2,1,0:T(8,128)(2,1)} %pad_maximum_fusion.1), calls=%async_computation.1 | async-start | bytes 6291456 | tf_op jit(solution)/shard_map/all_to_all | solution.py:512
  708.5 725.7 %copy-start.1 = (s32[4,512]{1,0:T(4,128)S(1)}, s32[4,512]{1,0:T(4,128)}, u32[]{:S(2)}) copy-start(s32[4,512]{1,0:T(4,128)} %param.17) | copy-start | bytes 24580
  (25 other events, 50.1 us)
Sparse Core Ops, SparseCore 0:
  10.9 61.7 all-gather.12
  75.5 74.1 all-gather.14
  152.6 73.3 all-gather.16
  228.7 65.4 all-gather.18
  297.5 67.9 all-gather.10
  454.7 136.5 reduce-scatter.13
  593.6 135.2 reduce-scatter.11
  731.1 133.8 reduce-scatter.7
  867.3 133.8 reduce-scatter.9
  1003.3 141.6 reduce-scatter.19
  1147.2 141.5 reduce-scatter.15
  1291.0 141.4 reduce-scatter.17

commit v2 on v1

--- a/solution.py
+++ b/solution.py
@@ -1,6 +1,8 @@
 import jax
 import jax.numpy as jnp
 from jax import lax
+from jax.experimental import pallas as pl
+from jax.experimental.pallas import tpu as pltpu
 from jax.sharding import PartitionSpec as P
 
 D = 1024
@@ -330,6 +332,535 @@
     )
 
 
+MESH_IDS = pl.DeviceIdType.MESH
+Z_SIZE = 4
+FIRST_X = (0, 3)
+
+
+def chip_coordinates():
+    row, col = lax.axis_index("row"), lax.axis_index("col")
+    return row // 2, row % 2, col // 2, col % 2
+
+
+def device_of(z, x, y, core):
+    return (z * 2 + x, y * 2 + core)
+
+
+def greet(z, x, y, core):
+    barrier = pltpu.get_barrier_semaphore()
+
+    def signal(target):
+        pl.semaphore_signal(barrier, inc=1, device_id=target, device_id_type=MESH_IDS)
+
+    signal(device_of(z, 1 - x, y, core))
+    signal(device_of(z, x, 1 - y, core))
+    signal(device_of(z, x, y, 1 - core))
+
+    for step in range(1, Z_SIZE):
+        signal(device_of((z + step) % Z_SIZE, x, y, core))
+    pl.semaphore_wait(barrier, 3 + Z_SIZE - 1)
+
+
+def gather_kernel(*refs):
+    count = len(FIRST_X) + 2
+    shards, wholes = refs[:count], refs[count : 2 * count]
+    own_sem, link_recv, core_recv, send_sem = refs[2 * count :]
+    z, x, y, core = chip_coordinates()
+    greet(z, x, y, core)
+
+    def spot(array, pz, px, py, pcore):
+        return wholes[array].at[py * 2 + pcore, :, pl.ds((pz * 2 + px) * 128, 128)]
+
+    def chip_id(pz, px, py):
+        return (pz * 2 + px) * 2 + py
+
+    def link(array, pz, px, py, way, target, own=False):
+        src = shards[array] if own else spot(array, pz, px, py, core)
+        return pltpu.make_async_remote_copy(
+            src_ref=src,
+            dst_ref=spot(array, pz, px, py, core),
+            send_sem=send_sem.at[array, way, chip_id(pz, px, py)],
+            recv_sem=link_recv.at[array, chip_id(pz, px, py)],
+            device_id=target,
+            device_id_type=MESH_IDS,
+        )
+
+    def twin(array, pz, px, py, own=False):
+        src = shards[array] if own else spot(array, pz, px, py, core)
+        return pltpu.make_async_remote_copy(
+            src_ref=src,
+            dst_ref=spot(array, pz, px, py, core),
+            send_sem=send_sem.at[array, 4, chip_id(pz, px, py)],
+            recv_sem=core_recv.at[array, chip_id(pz, px, py)],
+            device_id=device_of(z, x, y, 1 - core),
+            device_id_type=MESH_IDS,
+        )
+
+    x_mate, y_mate = device_of(z, 1 - x, y, core), device_of(z, x, 1 - y, core)
+    up, down = device_of(z + 1, x, y, core), device_of(z - 1, x, y, core)
+
+    def across(array, pz, px, py, leg, own=False):
+        if (array in FIRST_X) == (leg == 0):
+            return link(array, pz, px, py, 2, x_mate, own)
+        return link(array, pz, px, py, 3, y_mate, own)
+
+    order = (0, 1, 2, 3)
+    place_own = []
+    for array in order:
+        keep = pltpu.make_async_copy(shards[array], spot(array, z, x, y, core), own_sem.at[array])
+        keep.start()
+        place_own.append(keep)
+
+        @pl.when(z < Z_SIZE - 1)
+        def _():
+            link(array, z, x, y, 0, up, True).start()
+
+        @pl.when(z > 0)
+        def _():
+            link(array, z, x, y, 1, down, True).start()
+
+        across(array, z, x, y, 0, True).start()
+        twin(array, z, x, y, True).start()
+
+    def second(array, pz):
+        if array in FIRST_X:
+            arrived, onward = (1 - x, y), (3, y_mate)
+        else:
+            arrived, onward = (x, 1 - y), (2, x_mate)
+        moved = link(array, pz, *arrived, *onward)
+        moved.wait_recv()
+        moved.start()
+        twin(array, pz, *arrived).start()
+
+    def second_own(array, pz, own):
+        across(array, pz, x, y, 1, own).start()
+
+    for array in order:
+        second_own(array, z, True)
+        second(array, z)
+    for step in range(1, Z_SIZE):
+        for array in order:
+
+            @pl.when(z >= step)
+            def _():
+                pz = z - step
+                link(array, pz, x, y, 0, up).wait_recv()
+
+                @pl.when(z < Z_SIZE - 1)
+                def _():
+                    link(array, pz, x, y, 0, up).start()
+
+                across(array, pz, x, y, 0).start()
+                twin(array, pz, x, y).start()
+
+            @pl.when(z + step <= Z_SIZE - 1)
+            def _():
+                pz = z + step
+                link(array, pz, x, y, 1, down).wait_recv()
+
+                @pl.when(z > 0)
+                def _():
+                    link(array, pz, x, y, 1, down).start()
+
+                across(array, pz, x, y, 0).start()
+                twin(array, pz, x, y).start()
+
+        for array in order:
+
+            @pl.when(z >= step)
+            def _():
+                second_own(array, z - step, False)
+                second(array, z - step)
+
+            @pl.when(z + step <= Z_SIZE - 1)
+            def _():
+                second_own(array, z + step, False)
+                second(array, z + step)
+
+    def last(array, pz):
+        far = ((x, 1 - y), (1 - x, 1 - y)) if array in FIRST_X else ((1 - x, y), (1 - x, 1 - y))
+        for px, py in far:
+            link(array, pz, px, py, 2, x_mate).wait_recv()
+            twin(array, pz, px, py).start()
+
+    for array in order:
+        for pz in range(Z_SIZE):
+            last(array, pz)
+    for array in order:
+        place_own[array].wait()
+        for pz in range(Z_SIZE):
+            for px in range(2):
+                for py in range(2):
+                    twin(array, pz, px, py).wait()
+            link(array, pz, x, y, 2, x_mate).wait_send()
+            link(array, pz, x, y, 3, y_mate).wait_send()
+            if array in FIRST_X:
+                link(array, pz, 1 - x, y, 3, y_mate).wait_send()
+            else:
+                link(array, pz, x, 1 - y, 2, x_mate).wait_send()
+
+            @pl.when((z >= pz) & (z < Z_SIZE - 1))
+            def _():
+                link(array, pz, x, y, 0, up).wait_send()
+
+            @pl.when((z <= pz) & (z > 0))
+            def _():
+                link(array, pz, x, y, 1, down).wait_send()
+
+
+def gather_tiles(shards):
+    any_space = pl.BlockSpec(memory_space=pl.ANY)
+    count = len(shards)
+    return pl.pallas_call(
+        gather_kernel,
+        out_shape=[jax.ShapeDtypeStruct((4, s.shape[0], 1024), s.dtype) for s in shards],
+        in_specs=[any_space] * count,
+        out_specs=[any_space] * count,
+        scratch_shapes=[
+            pltpu.SemaphoreType.DMA((count,)),
+            pltpu.SemaphoreType.DMA((count, 16)),
+            pltpu.SemaphoreType.DMA((count, 16)),
+            pltpu.SemaphoreType.DMA((count, 5, 16)),
+        ],
+        compiler_params=pltpu.CompilerParams(
+            collective_id=0, has_side_effects=True, vmem_limit_bytes=4 << 20
+        ),
+        name="gather_tiles",
+    )(*shards)
+
+
+def add_rows(target, terms, low):
+    rows = 64
+
+    def chunk(index, carry):
+        at = pl.ds(pl.multiple_of(index * rows, rows), rows)
+        total = terms[0][at, :].astype(jnp.float32)
+        for term in terms[1:]:
+            total = total + term[at, :].astype(jnp.float32)
+        target[at, :] = total.astype(jnp.bfloat16) if low else total
+        return carry
+
+    lax.fori_loop(0, target.shape[0] // rows, chunk, 0)
+
+
+def scatter_kernel(*refs):
+    count = 4
+    gain_ref, gain_out, gain_held, gain_in, gain_line, gain_send, gain_recv = (
+        refs[count],
+        refs[2 * count + 1],
+        *refs[-5:],
+    )
+    refs = refs[:count] + refs[count + 1 : 2 * count + 1] + refs[2 * count + 2 : -5]
+    wholes, outs = refs[:count], refs[count : 2 * count]
+    held, twins, firsts, seconds, lines, totals = (
+        refs[2 * count + count * k : 3 * count + count * k] for k in range(6)
+    )
+    load_sem, twin_send, twin_recv, link_send, link_recv, line_send, line_recv, out_sem = refs[
+        8 * count :
+    ]
+    z, x, y, core = chip_coordinates()
+    greet(z, x, y, core)
+    x_mate, y_mate = device_of(z, 1 - x, y, core), device_of(z, x, 1 - y, core)
+    up, down = device_of(z + 1, x, y, core), device_of(z - 1, x, y, core)
+
+    def spot(array, pz, px, py, pcore):
+        return wholes[array].at[py * 2 + pcore, :, pl.ds((pz * 2 + px) * 128, 128)]
+
+    def chip_id(pz, px, py):
+        return (pz * 2 + px) * 2 + py
+
+    def load(array, pz, px, py):
+        index = chip_id(pz, px, py)
+        return pltpu.make_async_copy(
+            spot(array, pz, px, py, core), held[array].at[index], load_sem.at[array, index]
+        )
+
+    def twin(array, pz, px, py):
+        index = chip_id(pz, px, py)
+        return pltpu.make_async_remote_copy(
+            src_ref=spot(array, pz, px, py, 1 - core),
+            dst_ref=twins[array].at[index],
+            send_sem=twin_send.at[array, index],
+            recv_sem=twin_recv.at[array, index],
+            device_id=device_of(z, x, y, 1 - core),
+            device_id_type=MESH_IDS,
+        )
+
+    def send(array, pz, px, py, inbox, slot, send_at, recv_at, target):
+        return pltpu.make_async_remote_copy(
+            src_ref=held[array].at[chip_id(pz, px, py)],
+            dst_ref=inbox[array].at[slot],
+            send_sem=send_at,
+            recv_sem=recv_at,
+            device_id=target,
+            device_id_type=MESH_IDS,
+        )
+
+    def first(array, pz, same):
+        if array in FIRST_X:
+            px, py, target = (x if same else 1 - x), 1 - y, y_mate
+        else:
+            px, py, target = 1 - x, (y if same else 1 - y), x_mate
+        slot = pz * 2 + same
+        return (px, py), send(
+            array,
+            pz,
+            px,
+            py,
+            firsts,
+            slot,
+            link_send.at[array, slot],
+            link_recv.at[array, slot],
+            target,
+        )
+
+    def second(array, pz):
+        px, py, target = (1 - x, y, x_mate) if array in FIRST_X else (x, 1 - y, y_mate)
+        return (px, py), send(
+            array,
+            pz,
+            px,
+            py,
+            seconds,
+            pz,
+            link_send.at[array, 8 + pz],
+            link_recv.at[array, 8 + pz],
+            target,
+        )
+
+    def line(array, pz, upward, slot):
+        return send(
+            array,
+            pz,
+            x,
+            y,
+            lines,
+            slot,
+            line_send.at[array, pz],
+            line_recv.at[array, slot],
+            up if upward else down,
+        )
+
+    gain_mates = (device_of(z, x, y, 1 - core), x_mate, y_mate)
+
+    def gain_copy(step):
+        return pltpu.make_async_remote_copy(
+            src_ref=gain_held.at[step],
+            dst_ref=gain_in.at[step],
+            send_sem=gain_send.at[step],
+            recv_sem=gain_recv.at[step],
+            device_id=gain_mates[step],
+            device_id_type=MESH_IDS,
+        )
+
+    def gain_across(step):
+        return pltpu.make_async_remote_copy(
+            src_ref=gain_held.at[3],
+            dst_ref=gain_line.at[step - 1],
+            send_sem=gain_send.at[2 + step],
+            recv_sem=gain_recv.at[2 + step],
+            device_id=device_of((z + step) % Z_SIZE, x, y, core),
+            device_id_type=MESH_IDS,
+        )
+
+    def gain_add(step):
+        gain_copy(step).wait_recv()
+        gain_held[step + 1] = gain_held[step] + gain_in[step]
+        if step < 2:
+            gain_copy(step + 1).start()
+        else:
+            for away in range(1, Z_SIZE):
+                gain_across(away).start()
+
+    def gain_finish():
+        for away in range(1, Z_SIZE):
+            gain_across(away).wait_recv()
+        total = None
+        for pz in range(Z_SIZE):
+            term = jnp.where(z == pz, gain_held[3], 0.0)
+            for away in range(1, Z_SIZE):
+                sender = (z + Z_SIZE - away) % Z_SIZE
+                term = jnp.where(sender == pz, gain_line[away - 1], term)
+            total = term if total is None else total + term
+        gain_out[...] = total
+        for step in range(3):
+            gain_copy(step).wait_send()
+        for away in range(1, Z_SIZE):
+            gain_across(away).wait_send()
+
+    gain_held[0] = gain_ref[...]
+    gain_copy(0).start()
+    order = (1, 3, 2, 0)
+
+    def begin(array, pz, px, py):
+        load(array, pz, px, py).start()
+        twin(array, pz, px, py).start()
+
+    spread = (0, 3, 1, 2)
+    for same in (0, 1):
+        for pz in spread:
+            for array in order:
+                px, py = (
+                    ((x if same else 1 - x), 1 - y)
+                    if array in FIRST_X
+                    else (1 - x, (y if same else 1 - y))
+                )
+                begin(array, pz, px, py)
+    for pz in spread:
+        for array in order:
+            px, py = (1 - x, y) if array in FIRST_X else (x, 1 - y)
+            begin(array, pz, px, py)
+    for pz in spread:
+        for array in order:
+            begin(array, pz, x, y)
+
+    def arrive(array, pz, px, py):
+        load(array, pz, px, py).wait()
+        twin(array, pz, px, py).wait_recv()
+        index = chip_id(pz, px, py)
+        return held[array].at[index], twins[array].at[index]
+
+    for same in (0, 1):
+        for pz in spread:
+            for array in order:
+                (px, py), moved = first(array, pz, same)
+                mine, other = arrive(array, pz, px, py)
+                add_rows(mine, (mine, other), True)
+                moved.start()
+        gain_add(same)
+    for pz in spread:
+        for array in order:
+            (px, py), moved = second(array, pz)
+            mine, other = arrive(array, pz, px, py)
+            first(array, pz, 0)[1].wait_recv()
+            add_rows(mine, (mine, other, firsts[array].at[pz * 2]), True)
+            moved.start()
+
+    gain_add(2)
+
+    def terms_of(array, pz):
+        mine, other = arrive(array, pz, x, y)
+        first(array, pz, 1)[1].wait_recv()
+        second(array, pz)[1].wait_recv()
+        return mine, (mine, other, firsts[array].at[pz * 2 + 1], seconds[array].at[pz])
+
+    for step in range(Z_SIZE - 1, 0, -1):
+        for array in order:
+
+            @pl.when(z + step <= Z_SIZE - 1)
+            def _():
+                pz = z + step
+                mine, terms = terms_of(array, pz)
+                moved = line(array, pz, True, step - 1)
+
+                @pl.when(z == 0)
+                def _():
+                    add_rows(mine, terms, True)
+
+                @pl.when(z > 0)
+                def _():
+                    line(array, pz, True, step).wait_recv()
+                    add_rows(mine, terms + (lines[array].at[step],), True)
+
+                moved.start()
+
+            @pl.when(z >= step)
+            def _():
+                pz = z - step
+                mine, terms = terms_of(array, pz)
+                moved = line(array, pz, False, Z_SIZE + step - 1)
+
+                @pl.when(z == Z_SIZE - 1)
+                def _():
+                    add_rows(mine, terms, True)
+
+                @pl.when(z < Z_SIZE - 1)
+                def _():
+                    line(array, pz, False, Z_SIZE + step).wait_recv()
+                    add_rows(mine, terms + (lines[array].at[Z_SIZE + step],), True)
+
+                moved.start()
+
+    for array in order:
+        mine, terms = terms_of(array, z)
+        from_below, from_above = lines[array].at[0], lines[array].at[Z_SIZE]
+
+        @pl.when(z == 0)
+        def _():
+            line(array, z, False, Z_SIZE).wait_recv()
+            add_rows(totals[array], terms + (from_above,), False)
+
+        @pl.when(z == Z_SIZE - 1)
+        def _():
+            line(array, z, True, 0).wait_recv()
+            add_rows(totals[array], terms + (from_below,), False)
+
+        @pl.when((z > 0) & (z < Z_SIZE - 1))
+        def _():
+            line(array, z, True, 0).wait_recv()
+            line(array, z, False, Z_SIZE).wait_recv()
+            add_rows(totals[array], terms + (from_below, from_above), False)
+
+        pltpu.make_async_copy(totals[array], outs[array], out_sem.at[array]).start()
+
+    gain_finish()
+    for array in order:
+        pltpu.make_async_copy(totals[array], outs[array], out_sem.at[array]).wait()
+        for pz in range(Z_SIZE):
+            for px in range(2):
+                for py in range(2):
+                    twin(array, pz, px, py).wait_send()
+            first(array, pz, 0)[1].wait_send()
+            first(array, pz, 1)[1].wait_send()
+            second(array, pz)[1].wait_send()
+
+            @pl.when(z != pz)
+            def _():
+                line(array, pz, True, 0).wait_send()
+
+
+def scatter_tiles(wholes, gains):
+    any_space = pl.BlockSpec(memory_space=pl.ANY)
+    count = len(wholes)
+    sizes = [w.shape[1] for w in wholes]
+
+    def boxes(slots, kind=jnp.bfloat16):
+        return [pltpu.VMEM((slots, n, 128), kind) for n in sizes]
+
+    return pl.pallas_call(
+        scatter_kernel,
+        out_shape=[jax.ShapeDtypeStruct((n, 128), jnp.float32) for n in sizes]
+        + [jax.ShapeDtypeStruct(gains.shape, jnp.float32)],
+        in_specs=[any_space] * count + [pl.BlockSpec(memory_space=pltpu.VMEM)],
+        out_specs=[any_space] * count + [pl.BlockSpec(memory_space=pltpu.VMEM)],
+        scratch_shapes=boxes(16)
+        + boxes(16)
+        + boxes(8)
+        + boxes(4)
+        + boxes(8)
+        + [pltpu.VMEM((n, 128), jnp.float32) for n in sizes]
+        + [
+            pltpu.SemaphoreType.DMA((count, 16)),
+            pltpu.SemaphoreType.DMA((count, 16)),
+            pltpu.SemaphoreType.DMA((count, 16)),
+            pltpu.SemaphoreType.DMA((count, 12)),
+            pltpu.SemaphoreType.DMA((count, 12)),
+            pltpu.SemaphoreType.DMA((count, 4)),
+            pltpu.SemaphoreType.DMA((count, 8)),
+            pltpu.SemaphoreType.DMA((count,)),
+            pltpu.VMEM((4,) + gains.shape, jnp.float32),
+            pltpu.VMEM((3,) + gains.shape, jnp.float32),
+            pltpu.VMEM((3,) + gains.shape, jnp.float32),
+            pltpu.SemaphoreType.DMA((6,)),
+            pltpu.SemaphoreType.DMA((6,)),
+        ],
+        compiler_params=pltpu.CompilerParams(
+            collective_id=1, has_side_effects=True, vmem_limit_bytes=56 << 20
+        ),
+        name="scatter_tiles",
+    )(*wholes, gains)
+
+
 def slot_body(
     hidden_in,
     first_values,
@@ -352,33 +883,14 @@
     hidden_tile = w_gate.shape[1]
     column = lax.axis_index("col")
     score_scale = HEAD_DIM ** (-0.5)
-    both = ("row", "col")
-
-    def gather(tile):
-        return lax.all_gather(tile, both, axis=0, tiled=False)
-
-    row_count = width // w_query.shape[0]
-
-    def by_rows(whole, count_out):
-        tile_rows, tile_cols = whole.shape[1:]
-        whole = whole.reshape(row_count, slots, tile_rows, tile_cols)
-        return jnp.transpose(whole, (0, 2, 1, 3)).reshape(row_count * tile_rows, count_out)
-
-    def by_cols(whole, count_in):
-        tile_rows, tile_cols = whole.shape[1:]
-        whole = whole.reshape(row_count, slots, tile_rows, tile_cols)
-        return jnp.transpose(whole, (1, 2, 0, 3)).reshape(count_in, row_count * tile_cols)
-
     ff = hidden_tile * slots
     wide = w_query.shape[1]
-    qkv_tiles = gather(jnp.concatenate([w_query, w_key, w_value], axis=1))
-    wq = by_rows(qkv_tiles[:, :, :wide], width)
-    wk = by_rows(qkv_tiles[:, :, wide : 2 * wide], width)
-    wv = by_rows(qkv_tiles[:, :, 2 * wide :], width)
-    wo = by_cols(gather(w_out), width)
-    wg = by_rows(gather(w_gate), ff)
-    wu = by_rows(gather(w_up), ff)
-    wd = by_cols(gather(w_down), ff)
+    near = jnp.concatenate([w_query.T, w_key.T, w_value.T, w_out], axis=0)
+    near_all, gate_all, up_all, down_all = gather_tiles((near, w_gate.T, w_up.T, w_down))
+    wq, wk, wv, wo = (
+        near_all[:, k * wide : (k + 1) * wide].reshape(width, width) for k in range(4)
+    )
+    wg, wu, wd = (whole.reshape(ff, width) for whole in (gate_all, up_all, down_all))
 
     first_rows = jnp.transpose(first_values, (0, 2, 1))
     feature_tile = first_rows.shape[2]
@@ -405,9 +917,9 @@
     scale_one = lax.rsqrt(jnp.mean(hidden * hidden, axis=1, keepdims=True) + EPSILON)
     normed_one = (hidden * scale_one * gain_attn).astype(jnp.bfloat16)
     by_head = (count, heads, HEAD_DIM)
-    queries = rotate(product(normed_one, wq).reshape(by_head), cosine, sine).astype(jnp.bfloat16)
-    keys = rotate(product(normed_one, wk).reshape(by_head), cosine, sine).astype(jnp.bfloat16)
-    values = (0.5 * product(normed_one, wv) + 0.5 * first).astype(jnp.bfloat16).reshape(by_head)
+    queries = rotate(product_right(normed_one, wq).reshape(by_head), cosine, sine).astype(jnp.bfloat16)
+    keys = rotate(product_right(normed_one, wk).reshape(by_head), cosine, sine).astype(jnp.bfloat16)
+    values = (0.5 * product_right(normed_one, wv) + 0.5 * first).astype(jnp.bfloat16).reshape(by_head)
 
     raw_scores = jnp.einsum("qhd,khd->hqk", queries, keys, preferred_element_type=jnp.float32)
     scores = jnp.where(allowed[None], raw_scores * score_scale, MASKED)
@@ -423,38 +935,26 @@
     mid = hidden + product(attended, wo)
     scale_two = lax.rsqrt(jnp.mean(mid * mid, axis=1, keepdims=True) + EPSILON)
     normed_two = (mid * scale_two * gain_ffn).astype(jnp.bfloat16)
-    gate_raw = product(normed_two, wg)
-    up_raw = product(normed_two, wu)
+    gate_raw = product_right(normed_two, wg)
+    up_raw = product_right(normed_two, wu)
     sigmoid_gate = jax.nn.sigmoid(gate_raw)
     silu_gate = gate_raw * sigmoid_gate
     hidden_act = (silu_gate * up_raw).astype(jnp.bfloat16)
     stored_out = (mid + product(hidden_act, wd)).astype(jnp.bfloat16)
 
-    def scatter(tiles):
-        tiles = tiles.reshape((row_count * slots,) + tiles.shape[2:])
-        return lax.psum_scatter(tiles, both, scatter_dimension=0, tiled=False).astype(jnp.float32)
-
-    def tiles_by_rows(grad):
-        depth, across = grad.shape
-        grad = grad.astype(jnp.bfloat16)
-        grad = grad.reshape(row_count, depth // row_count, slots, across // slots)
-        return scatter(jnp.transpose(grad, (0, 2, 1, 3)))
-
-    def tiles_by_cols(grad):
-        depth, across = grad.shape
-        grad = grad.astype(jnp.bfloat16)
-        grad = grad.reshape(slots, depth // slots, row_count, across // row_count)
-        return scatter(jnp.transpose(grad, (2, 0, 1, 3)))
-
-    grad_down = tiles_by_cols(product_left(hidden_act, grad_rows))
+    def pieces(left, right):
+        grad = product_left(left, right).astype(jnp.bfloat16)
+        return grad.reshape(slots, grad.shape[0] // slots, width)
+
+    grad_down = pieces(hidden_act, grad_rows)
     d_hidden = product_right(grad_rows, wd)
     d_gate = (d_hidden * up_raw * sigmoid_gate * (1.0 + gate_raw * (1.0 - sigmoid_gate))).astype(
         jnp.bfloat16
     )
     d_up = (d_hidden * silu_gate).astype(jnp.bfloat16)
-    grad_gate = tiles_by_rows(product_left(normed_two, d_gate))
-    grad_up = tiles_by_rows(product_left(normed_two, d_up))
-    d_normed_two = product_right(d_gate, wg) + product_right(d_up, wu)
+    grad_gate = pieces(d_gate, normed_two)
+    grad_up = pieces(d_up, normed_two)
+    d_normed_two = product(d_gate, wg) + product(d_up, wu)
     gain_sum_two = jnp.sum(d_normed_two * mid * scale_two, axis=0)
     scaled_two = d_normed_two * gain_ffn
     stat_two = jnp.sum(scaled_two * mid, axis=1, keepdims=True)
@@ -464,7 +964,7 @@
         - mid * (scale_two * scale_two * scale_two * stat_two / width)
     )
     d_branch = d_mid.astype(jnp.bfloat16)
-    grad_out = tiles_by_cols(product_left(attended, d_branch))
+    grad_out = pieces(attended, d_branch)
     d_attended = product_right(d_branch, wo).astype(jnp.bfloat16).reshape(by_head)
     d_probs = jnp.einsum("qhd,khd->hqk", d_attended, values, preferred_element_type=jnp.float32)
     inner_sum = jnp.sum(probs * d_probs, axis=-1, keepdims=True)
@@ -483,13 +983,13 @@
     d_value_proj = (0.5 * d_values.astype(jnp.float32)).astype(jnp.bfloat16)
     d_query_raw = rotate_back(d_query, cosine, sine).astype(jnp.bfloat16).reshape(count, width)
     d_key_raw = rotate_back(d_key, cosine, sine).astype(jnp.bfloat16).reshape(count, width)
-    grad_query = tiles_by_rows(product_left(normed_one, d_query_raw))
-    grad_key = tiles_by_rows(product_left(normed_one, d_key_raw))
-    grad_value = tiles_by_rows(product_left(normed_one, d_value_proj))
+    grad_query = pieces(d_query_raw, normed_one)
+    grad_key = pieces(d_key_raw, normed_one)
+    grad_value = pieces(d_value_proj, normed_one)
     d_normed_one = (
-        product_right(d_query_raw, wq)
-        + product_right(d_key_raw, wk)
-        + product_right(d_value_proj, wv)
+        product(d_query_raw, wq)
+        + product(d_key_raw, wk)
+        + product(d_value_proj, wv)
     )
     gain_sum_one = jnp.sum(d_normed_one * hidden * scale_one, axis=0)
     scaled_one = d_normed_one * gain_attn
@@ -512,26 +1012,31 @@
     back = lax.all_to_all(sent_back, "col", split_axis=0, concat_axis=0, tiled=True)
     value_back = back[:, 2 * rows :].reshape(slots, rows, slots, feature_tile)
     value_back = jnp.transpose(value_back, (0, 3, 2, 1)).reshape(slots, feature_tile, count)
-    gain_grad_one, gain_grad_two = lax.psum((gain_sum_one, gain_sum_two), both)
+    grad_near = jnp.concatenate([grad_query, grad_key, grad_value, grad_out], axis=1)
+    gains = jnp.concatenate([gain_sum_one, gain_sum_two]).reshape(-1, 128)
+    near_tile, gate_tile, up_tile, down_tile, gain_total = scatter_tiles(
+        (grad_near, grad_gate, grad_up, grad_down), gains
+    )
+    gain_total = gain_total.reshape(2, width)
     return (
         back[:, :rows],
         back[:, rows : 2 * rows].astype(jnp.float32),
         value_back.astype(jnp.float32),
-        gain_grad_one,
-        gain_grad_two,
-        grad_query,
-        grad_key,
-        grad_value,
-        grad_out,
-        grad_gate,
-        grad_up,
-        grad_down,
+        gain_total[0],
+        gain_total[1],
+        near_tile[:wide].T,
+        near_tile[wide : 2 * wide].T,
+        near_tile[2 * wide : 3 * wide].T,
+        near_tile[3 * wide :],
+        gate_tile.T,
+        up_tile.T,
+        down_tile,
     )
 
 
 def solution(mesh):
     def body(*arrays):
-        one_each = arrays[0].shape[0] == mesh.shape["col"]
+        one_each = mesh.shape["row"] == 2 * Z_SIZE and arrays[0].shape[0] == mesh.shape["col"] == 4
         return (slot_body if one_each else tiled_body)(*arrays)
 
     return jax.shard_map(

time: 1450 us -> 547 us (0.38)
  waiting for transfers between devices: 993 us -> 0.01 us
  Pallas kernels: 0 us -> 316 us
  local copies, waits for them, and re-layouts: 169 us -> 51.1 us
  blocking collectives: 78 us -> 0 us
    reduce_scatter x7 -> x0, waiting for transfers between devices: 712 us -> none  [scatter(): lax.psum_scatter(tiles, both, scatter_dimension=0, tiled=False)]
    pallas_call x0 -> x2, Pallas kernels: none -> 316 us  [the longest x1 168 us: scatter_tiles(): pl.pallas_call(scatter_kernel, out_shape=[jax.ShapeDtypeStruct((n, 128),...]
    all_gather x5 -> x0, waiting for transfers between devices: 238 us -> none  [gather(): return lax.all_gather(tile, both, axis=0, tiled=False)]
    reshape x12 -> x1, local copies, waits for them, and re-layouts: 81.1 us -> 0.01 us  [the longest x5 38 us: tiles_by_rows(): grad = grad.reshape(row_count, depth // row_count, slots, across // slots)]
    psum x1 -> x0, blocking collectives: 78 us -> none  [slot_body(): gain_grad_one, gain_grad_two = lax.psum((gain_sum_one, gain_sum_two), both)]
    all_to_all x1, waiting for transfers between devices: 40.9 us -> 0.01 us  [slot_body(): got = lax.all_to_all(sent, 'col', split_axis=0, concat_axis=0, tiled=True)]
    transpose x12 -> x0, local copies, waits for them, and re-layouts: 40.8 us -> none  [the longest x5 26.3 us: tiles_by_rows(): return scatter(jnp.transpose(grad, (0, 2, 1, 3)))]
  transfers between devices with their start and end apart: 14 -> 2, of which waited for: 11 -> 0; matrix products, arithmetic and copies ran while one was open for 17% -> 4% of each run, Pallas kernels for 0% -> 58%
where the time goes in v2:
time: 547 us; the launch traced here: 541 us
  Pallas kernels  316 us (58%)
  matrix products  115 us (21%)
  local copies, waits for them, and re-layouts  51.1 us (9%)
  other arithmetic  48.1 us (9%)
  starting transfers between devices  8.65 us (2%)
    pallas_call x1, Pallas kernels, scatter_tiles(): pl.pallas_call(scatter_kernel, out_shape=[jax.ShapeDtypeStruct((n, 128),...  168 us
    pallas_call x1, Pallas kernels, gather_tiles(): pl.pallas_call(gather_kernel, out_shape=[jax.ShapeDtypeStruct((4, s.shape...  149 us
    dot_general x7, matrix products, product_right(): lax.dot_general(left, right, (((1,), (1,)), ((), ())), preferred_element_...  27.3 us
    dot_general x7, matrix products, product_left(): lax.dot_general(left, right, (((0,), (0,)), ((), ())), preferred_element_...  26.1 us
    unnamed x158, local copies, waits for them, and re-layouts  19.2 us
    dot_general x7, matrix products, product(): return jnp.dot(left, right, preferred_element_type=jnp.float32)  19.2 us
    dot_general x1, matrix products, slot_body(): jnp.einsum('qhd,khd->hqk', d_attended, values, preferred_element_type=jnp...  14.4 us
    convert_element_type x1, other arithmetic, slot_body(): d_scores = (probs * (d_probs - inner_sum)).astype(jnp.bfloat16)  12.5 us
  transfers between devices with their start and end apart: 2, of which 0 were waited for; matrix products, arithmetic and copies ran while one was open for 4% of the time, Pallas kernels for 58%

profile of v2, /device:TPU:0, one launch (start us, length us, event | category | flops | bytes accessed | tf_op | source)
XLA Modules:
  0.0 540.8 jit_solution(12171125406612785938)
XLA Ops:
  3.8 2.8 pad_maximum_fusion.1
  6.7 4.8 all-to-all-start
  12.2 148.8 %gather_tiles.1 = (bf16[4,1024,1024]{2,1,0:T(8,128)(2,1)S(1)}, bf16[4,704,1024]{2,1,0:T(8,128)(2,1)S(1)}, bf16[4,704,1024]{2,1,0:T(8,128)(2,1)S(1)}, bf16[4,704,1024]{2,1,0:T(8,128)(2,1)S(1)}) custom-call(bf16[1024,128]{1,0:T(8,128)(2,1)S(1)} %pad_maximum_fusion.11.refs_0_, bf16[704,128]{1,0:T(8,128)(2,1)S(1)} %bitcast.142, bf16[704,128]{1,0:T(8,128)(2,1)S(1)} %bitcast.143, ...), custom_call_target="tpu_custom_call" | custom-call | tf_op jit(solution)/shard_map/gather_tiles/pallas_call | solution.py:514
  161.0 2.4 copy-done.5
  163.4 2.5 copy-done.6
  165.9 2.4 copy-done.7
  169.2 3.2 fusion.30
  172.4 2.3 fusion.3
  180.9 7.3 %fusion = (f32[16,512]{1,0:T(8,128)S(1)}, f32[16,512,512]{1,2,0:T(8,128)}) fusion(pred[512,512]{0,1:T(8,128)(4,1)S(1)} %compare_and_fusion, bf16[512,16,32]{0,2,1:T(8,128)(2,1)S(1)} %get-tuple-element.97, bf16[512,16,32]{0,2,1:T(8,128)(2,1)S(1)} %get-tuple-element.98, bf16[512,16,32]{0,2,1:T(8,128)(2,1)S(1)} %get-tuple-element.88, ...), kind=kOutput, calls=%fused_computation.5 | convolution fusion | flops 553639936 | bytes 19169280 | tf_op jit(solution)/shard_map/qhd,khd->hqk/dot_general | solution.py:924
  188.2 9.4 %exponential_reduce_fusion = f32[16,512]{1,0:T(8,128)S(1)} fusion(f32[16,512,512]{1,2,0:T(8,128)} %get-tuple-element.106, f32[16,512]{1,0:T(8,128)S(1)} %get-tuple-element.105, pred[512,512]{0,1:T(8,128)(4,1)S(1)} %compare_and_fusion), kind=kLoop, calls=%fused_computation.3 | loop fusion | flops 16769024 | bytes 17104896 | tf_op jit(solution)/shard_map/reduce_sum | solution.py:927
  198.2 3.7 fusion.31
  201.9 2.5 reshape.439
  204.4 2.9 copy.64
  208.9 2.3 multiply_convert_fusion.6
  211.2 1.6 copy.65
  212.9 8.3 %convolution_convert_fusion.8 = bf16[16,64,512]{2,1,0:T(8,128)(2,1)S(1)} fusion(bf16[512,16,64]{0,2,1:T(8,128)(2,1)S(1)} %bitcast.169, f32[16,512,512]{1,2,0:T(8,128)} %get-tuple-element.106, f32[16,512]{1,0:T(8,128)S(1)} %copy-done.47, pred[512,512]{0,1:T(8,128)(4,1)S(1)} %compare_and_fusion), kind=kOutput, calls=%fused_computation.49 | convolution fusion | flops 554172416 | bytes 19169280 | tf_op jit(solution)/shard_map/hqk,khd->qhd/dot_general | solution.py:931
  223.9 5.0 fusion.35
  229.0 5.0 fusion.36
  234.0 10.2 %multiply_convert_fusion.3 = (bf16[512,2816]{1,0:T(8,128)(2,1)}, bf16[512,2816]{1,0:T(8,128)(2,1)S(1)}, bf16[512,2816]{1,0:T(8,128)(2,1)}) fusion(f32[512,2816]{1,0:T(8,128)} %fusion.35, f32[512,2816]{1,0:T(8,128)} %fusion.36, bf16[512,1024]{1,0:T(8,128)(2,1)} %copy-done.38, bf16[2816,1024]{1,0:T(8,128)(2,1)S(1)} %bitcast.152), kind=kOutput, calls=%fused_computation.10 | convolution fusion | flops 2974416896 | bytes 27000832 | tf_op jit(solution)/shard_map/dot_general | solution.py:29
  244.2 3.2 fusion.37
  247.7 3.6 multiply_reduce_fusion.1
  252.9 2.3 convolution_convert_fusion.9
  255.2 2.3 copy.67
  257.5 14.4 %multiply_reduce_fusion = (f32[16,512]{1,0:T(8,128)S(1)}, f32[16,512,512]{1,2,0:T(8,128)}) fusion(f32[16,512,512]{1,2,0:T(8,128)} %get-tuple-element.106, f32[16,512]{1,0:T(8,128)} %log_add_fusion, pred[512,512]{0,1:T(8,128)(4,1)S(1)} %compare_and_fusion, bf16[512,16,64]{0,2,1:T(8,128)(2,1)} %bitcast.171, bf16[512,16,64]{0,2,1:T(8,128)(2,1)S(1)} %bitcast.170), kind=kOutput, calls=%fused_computation.1 | convolution fusion | flops 557834240 | bytes 35979264 | tf_op jit(solution)/shard_map/qhd,khd->hqk/dot_general | solution.py:969
  271.9 12.5 %multiply_convert_fusion = bf16[16,512,512]{1,2,0:T(8,128)(2,1)S(1)} fusion(f32[16,512,512]{1,2,0:T(8,128)} %get-tuple-element.111, f32[16,512,512]{1,2,0:T(8,128)} %get-tuple-element.106, f32[16,512]{1,0:T(8,128)S(1)} %get-tuple-element.110, f32[16,512]{1,0:T(8,128)S(1)} %copy-done.48, pred[512,512]{0,1:T(8,128)(4,1)S(1)} %compare_and_fusion), kind=kLoop, calls=%fused_computation | loop fusion | flops 25165824 | bytes 42270720 | tf_op jit(solution)/shard_map/convert_element_type | solution.py:971
  286.0 2.6 multiply_bitcast_fusion
  288.6 8.1 %multiply_convert_fusion.4 = bf16[16,64,512]{2,1,0:T(8,128)(2,1)S(1)} fusion(bf16[512,16,64]{0,2,1:T(8,128)(2,1)S(1)} %bitcast.172, f32[16,512,512]{1,2,0:T(8,128)} %get-tuple-element.106, f32[16,512]{1,0:T(8,128)S(1)} %copy-done.48, pred[512,512]{0,1:T(8,128)(4,1)S(1)} %compare_and_fusion), kind=kOutput, calls=%fused_computation.33 | convolution fusion | flops 555745280 | bytes 19169280 | tf_op jit(solution)/shard_map/hqk,qhd->khd/dot_general | solution.py:979
  296.8 5.0 convolution_convert_fusion.2
  301.8 5.3 convolution_convert_fusion.1
  307.2 2.6 convolution_convert_fusion.3
  311.8 2.6 convolution_convert_fusion.5
  315.7 2.6 convolution_convert_fusion.6
  320.7 4.1 add_convert_fusion
  324.8 4.3 fusion.10
  330.2 2.7 copy.71
  333.0 1.5 reshape.428
  334.5 2.5 fusion.8
  337.1 1.8 pad_maximum_fusion.2
  338.9 3.9 all-to-all-start.1
  342.8 2.9 convolution_convert_fusion.4
  346.4 5.1 convolution_convert_fusion
  351.5 3.7 pad_maximum_fusion.refs_0_
  355.2 167.5 %scatter_tiles.1 = (f32[1024,128]{1,0:T(8,128)}, f32[704,128]{1,0:T(8,128)}, f32[704,128]{1,0:T(8,128)}, f32[704,128]{1,0:T(8,128)}, f32[16,128]{1,0:T(8,128)}) custom-call(bf16[4,1024,1024]{2,1,0:T(8,128)(2,1)} %pad_maximum_fusion.refs_0_, bf16[4,704,1024]{2,1,0:T(8,128)(2,1)} %bitcast.166, bf16[4,704,1024]{2,1,0:T(8,128)(2,1)} %bitcast.167, ...), custom_call_target="tpu_custom_call" | custom-call | tf_op jit(solution)/shard_map/scatter_tiles/pallas_call | solution.py:830
  522.7 1.8 fusion.32
  528.1 2.6 slice_convert_fusion
  530.7 2.2 reshape.440
  532.9 2.4 copy.72
  535.2 3.1 reshape.438
  (195 shorter events, 32.1 us)
Async XLA Ops:
  0.6 167.7 %copy-start = (s32[4,512]{1,0:T(4,128)S(1)}, s32[4,512]{1,0:T(4,128)}, u32[]{:S(2)}) copy-start(s32[4,512]{1,0:T(4,128)} %param.17) | copy-start | bytes 24580
  6.7 4.9 copy-start.59
  6.7 5.1 copy-start.49
  6.7 5.2 copy-start.50
  6.7 5.3 copy-start.51
  6.7 5.4 %copy-start.52 = (bf16[256,128]{1,0:T(8,128)(2,1)S(1)}, bf16[256,128]{1,0:T(8,128)(2,1)}, u32[]{:S(2)}) copy-start(bf16[256,128]{1,0:T(8,128)(2,1)} %param.23) | copy-start | bytes 196612
  6.7 5.4 %copy-start.2 = (bf16[128,704]{0,1:T(8,128)(2,1)S(1)}, bf16[128,704]{0,1:T(8,128)(2,1)}, u32[]{:S(2)}) copy-start(bf16[128,704]{0,1:T(8,128)(2,1)} %param.24) | copy-start | bytes 540676
  6.7 5.4 %copy-start.3 = (bf16[128,704]{0,1:T(8,128)(2,1)S(1)}, bf16[128,704]{0,1:T(8,128)(2,1)}, u32[]{:S(2)}) copy-start(bf16[128,704]{0,1:T(8,128)(2,1)} %param.25) | copy-start | bytes 540676
  6.7 5.4 %copy-start.4 = (bf16[704,128]{1,0:T(8,128)(2,1)S(1)}, bf16[704,128]{1,0:T(8,128)(2,1)}, u32[]{:S(2)}) copy-start(bf16[704,128]{1,0:T(8,128)(2,1)} %refs_3_.1) | copy-start | bytes 540676
  6.7 165.7 %all-to-all-start = ((bf16[4,384,1024]{2,1,0:T(8,128)(2,1)}), bf16[4,384,1024]{2,1,0:T(8,128)(2,1)}, u32[]{:S(2)}, u32[]{:S(2)}) async-start(bf16[4,384,1024]{2,1,0:T(8,128)(2,1)} %pad_maximum_fusion.1), calls=%async_computation | async-start | bytes 6291456 | tf_op jit(solution)/shard_map/all_to_all | solution.py:900
  169.2 6.1 %copy-start.56 = (f32[1024]{0:T(1024)S(1)}, f32[1024]{0:T(1024)}, u32[]{:S(2)}) copy-start(f32[1024]{0:T(1024)} %param.18) | copy-start | bytes 12292
  172.4 5.7 %copy-start.11 = (bf16[4,256,1024]{2,1,0:T(8,128)(2,1)}, bf16[4,256,1024]{2,1,0:T(8,128)(2,1)S(1)}, u32[]{:S(2)}) copy-start(bf16[4,256,1024]{2,1,0:T(8,128)(2,1)S(1)} %get-tuple-element.73) | copy-start | bytes 6291460
  176.8 31.0 %copy-start.35 = (bf16[4,128,1024]{2,1,0:T(8,128)(2,1)}, bf16[4,128,1024]{2,1,0:T(8,128)(2,1)S(1)}, u32[]{:S(2)}) copy-start(bf16[4,128,1024]{2,1,0:T(8,128)(2,1)S(1)} %fusion.5) | copy-start | bytes 3145732
  180.8 7.4 %copy-start.22 = (bf16[512,16,32]{0,2,1:T(8,128)(2,1)}, bf16[512,16,32]{0,2,1:T(8,128)(2,1)S(1)}, u32[]{:S(2)}) copy-start(bf16[512,16,32]{0,2,1:T(8,128)(2,1)S(1)} %get-tuple-element.87) | copy-start | bytes 1572868
  180.8 7.4 %copy-start.24 = (bf16[512,16,32]{0,2,1:T(8,128)(2,1)}, bf16[512,16,32]{0,2,1:T(8,128)(2,1)S(1)}, u32[]{:S(2)}) copy-start(bf16[512,16,32]{0,2,1:T(8,128)(2,1)S(1)} %get-tuple-element.88) | copy-start | bytes 1572868
  180.8 7.3 %copy-start.26 = (bf16[512,16,32]{0,2,1:T(8,128)(2,1)}, bf16[512,16,32]{0,2,1:T(8,128)(2,1)S(1)}, u32[]{:S(2)}) copy-start(bf16[512,16,32]{0,2,1:T(8,128)(2,1)S(1)} %get-tuple-element.97) | copy-start | bytes 1572868
  180.8 7.3 %copy-start.28 = (bf16[512,16,32]{0,2,1:T(8,128)(2,1)}, bf16[512,16,32]{0,2,1:T(8,128)(2,1)S(1)}, u32[]{:S(2)}) copy-start(bf16[512,16,32]{0,2,1:T(8,128)(2,1)S(1)} %get-tuple-element.98) | copy-start | bytes 1572868
  208.9 3.9 copy-start.47
  211.2 12.7 %slice-start.6 = ((s8[5767168]{0:T(1024)(128)(4,1)}), s8[1572864]{0:T(1024)(128)(4,1)S(1)}, s32[]{:S(2)}) async-start(s8[5767168]{0:T(1024)(128)(4,1)} %bitcast.154), calls=%async_computation.8 | async-start | bytes 3145728
  212.8 8.3 %copy-start.15 = (bf16[4,256,1024]{2,1,0:T(8,128)(2,1)S(1)}, bf16[4,256,1024]{2,1,0:T(8,128)(2,1)}, u32[]{:S(2)}) copy-start(bf16[4,256,1024]{2,1,0:T(8,128)(2,1)} %get-tuple-element.74) | copy-start | bytes 6291460
  212.9 8.3 %copy-start.20 = (bf16[4,128,1024]{2,1,0:T(8,128)(2,1)S(1)}, bf16[4,128,1024]{2,1,0:T(8,128)(2,1)}, u32[]{:S(2)}) copy-start(bf16[4,128,1024]{2,1,0:T(8,128)(2,1)} %get-tuple-element.82) | copy-start | bytes 3145732
  212.9 11.0 %slice-start.7 = ((s8[5767168]{0:T(1024)(128)(4,1)}), s8[4194304]{0:T(1024)(128)(4,1)S(1)}, s32[]{:S(2)}) async-start(s8[5767168]{0:T(1024)(128)(4,1)} %bitcast.154), calls=%async_computation.9 | async-start | bytes 8388608
  222.6 6.4 %slice-start = ((s8[5767168]{0:T(1024)(128)(4,1)}), s8[4194304]{0:T(1024)(128)(4,1)S(1)}, s32[]{:S(2)}) async-start(s8[5767168]{0:T(1024)(128)(4,1)} %bitcast.144), calls=%async_computation.2 | async-start | bytes 8388608
  222.9 6.1 %copy-start.38 = (bf16[512,1024]{1,0:T(8,128)(2,1)}, bf16[512,1024]{1,0:T(8,128)(2,1)S(1)}, u32[]{:S(2)}) copy-start(bf16[512,1024]{1,0:T(8,128)(2,1)S(1)} %multiply_convert_fusion.5) | copy-start | bytes 3145732
  223.9 5.1 slice-start.1
  223.9 5.1 copy-start.18
  223.9 10.0 %slice-start.4 = ((s8[5767168]{0:T(1024)(128)(4,1)}), s8[4194304]{0:T(1024)(128)(4,1)S(1)}, s32[]{:S(2)}) async-start(s8[5767168]{0:T(1024)(128)(4,1)} %bitcast.150), calls=%async_computation.6 | async-start | bytes 8388608
  229.0 5.0 slice-start.5
  257.5 14.4 %copy-start.48 = (f32[16,512]{1,0:T(8,128)S(1)}, f32[16,512]{1,0:T(8,128)}, u32[]{:S(2)}) copy-start(f32[16,512]{1,0:T(8,128)} %log_add_fusion) | copy-start | bytes 98308
  271.9 12.5 %copy-start.27 = (bf16[512,16,32]{0,2,1:T(8,128)(2,1)S(1)}, bf16[512,16,32]{0,2,1:T(8,128)(2,1)}, u32[]{:S(2)}) copy-start(bf16[512,16,32]{0,2,1:T(8,128)(2,1)} %copy-done.26) | copy-start | bytes 1572868
  271.9 12.6 %copy-start.29 = (bf16[512,16,32]{0,2,1:T(8,128)(2,1)S(1)}, bf16[512,16,32]{0,2,1:T(8,128)(2,1)}, u32[]{:S(2)}) copy-start(bf16[512,16,32]{0,2,1:T(8,128)(2,1)} %copy-done.28) | copy-start | bytes 1572868
  288.6 8.2 %copy-start.39 = (bf16[512,1024]{1,0:T(8,128)(2,1)S(1)}, bf16[512,1024]{1,0:T(8,128)(2,1)}, u32[]{:S(2)}) copy-start(bf16[512,1024]{1,0:T(8,128)(2,1)} %copy-done.38) | copy-start | bytes 3145732
  288.6 8.2 %copy-start.65 = (bf16[512,2816]{1,0:T(8,128)(2,1)S(1)}, bf16[512,2816]{1,0:T(8,128)(2,1)}, u32[]{:S(2)}) copy-start(bf16[512,2816]{1,0:T(8,128)(2,1)} %copy-done.64) | copy-start | bytes 8650756
  296.8 32.3 %copy-start.37 = (bf16[16,64,512]{2,1,0:T(8,128)(2,1)}, bf16[16,64,512]{2,1,0:T(8,128)(2,1)S(1)}, u32[]{:S(2)}) copy-start(bf16[16,64,512]{2,1,0:T(8,128)(2,1)S(1)} %multiply_convert_fusion.4) | copy-start | bytes 3145732
  296.8 5.0 copy-start.63
  301.8 5.3 copy-start.42
  311.8 7.8 %slice-start.2 = ((s8[5767168]{0:T(1024)(128)(4,1)}), s8[4194304]{0:T(1024)(128)(4,1)S(1)}, s32[]{:S(2)}) async-start(s8[5767168]{0:T(1024)(128)(4,1)} %bitcast.147), calls=%async_computation.4 | async-start | bytes 8388608
  315.7 3.9 slice-start.3
  320.7 4.1 copy-start.31
  320.7 4.1 copy-start.57
  320.7 4.1 copy-start.58
  324.8 4.3 copy-start.54
  338.9 189.2 %all-to-all-start.1 = ((bf16[4,384,1024]{2,1,0:T(8,128)(2,1)}), bf16[4,384,1024]{2,1,0:T(8,128)(2,1)S(1)}, u32[]{:S(2)}, u32[]{:S(2)}) async-start(bf16[4,384,1024]{2,1,0:T(8,128)(2,1)} %pad_maximum_fusion.2), calls=%async_computation.1 | async-start | bytes 6291456 | tf_op jit(solution)/shard_map/all_to_all | solution.py:1012
  346.4 5.1 copy-start.32
  346.4 5.1 copy-start.33
  346.4 5.1 copy-start.34
  535.2 4.6 copy-start.44
  535.2 5.4 copy-start.1
  (28 other events, 68.6 us)
